TPU v7x, 128 devices: a whole 4x4x4 slice. The times are simulated.
128 devices in a mesh: act: 4 (over y), virt: 32 (over x, z, core).
Axes of the slice: x: 4, y: 4, z: 4, core: 2. Of those that a mesh axis runs over, the one named last changes fastest.
Arguments:
- amplitudes: bfloat16 [400, 640, 640], P('act', 'virt'), may hold values from -6 to 6
- virtual_fock_block: bfloat16 [640, 640], replicated, may hold values from -1 to 3.1, as said below
- metric: bfloat16 [400, 400], replicated, may hold values from -3.5 to 3.5, as said below
- active_block: bfloat16 [400, 400], replicated, may hold values from -0.3125 to 0.3125
Outputs:
- residual_vec: bfloat16 [400, 640, 640], P('act', 'virt')
- rayleigh: float32 [], replicated
- res_norm: float32 [], replicated
Inputs may be any that keep to these rules, and one draw needn't show every extreme that they name: `virtual_fock_block`: symmetric. `metric`: symmetric positive definite.
All inputs are finite; a program needn't handle non-finite values.
Results may differ from a plain program's by a relative error of at most 0.0099.
Values may be sent and summed in bfloat16 or wider, within the bound.
A program may use at most 128 MiB of HBM per device.

v0:
```python
import functools

import jax
import jax.numpy as jnp
from jax import lax
from jax.experimental import pallas as pl
from jax.experimental.pallas import tpu as pltpu
from jax.sharding import PartitionSpec as P

MESH = pl.DeviceIdType.MESH
AHEAD = 4


def stage_kernel(first, peers, groups, pair_count, start, *refs):
    if first:
        (shift_ref, fock_ref, metric_ref, active_ref, image_ref, rows_ref,
         left_ref, back_ref, kept_ref, early_ref) = refs[:10]
        *scratch, early_sent, early_landed = refs[10:]
    else:
        fock_ref, metric_ref, kept_ref, image_ref, rows_ref, left_ref, back_ref = refs[:7]
        scratch = refs[7:]
    (held, made, row_held, row_made, sent, landed, back_sent, back_landed,
     row_sent, row_landed, row_back_sent, row_back_landed) = scratch
    group = lax.axis_index("act")
    me = lax.axis_index("virt")
    rounds, rows, width = held.shape[0], held.shape[2], held.shape[3]
    items = row_held.shape[0]
    per_step = -(-items // rounds)
    barrier = pltpu.get_barrier_semaphore()
    for step in range(1, peers):
        pl.semaphore_signal(
            barrier, inc=1, device_id=(group, lax.rem(me + step, peers)), device_id_type=MESH)
    for step in range(1, groups):
        pl.semaphore_signal(
            barrier, inc=1, device_id=(lax.rem(group + step, groups), me), device_id_type=MESH)
    pl.semaphore_wait(barrier, peers + groups - 2)

    whole_rounds = pair_count // peers
    spare = pair_count % peers
    stride = peers // spare if spare and peers % spare == 0 else 1

    def pair_of(r, owner):
        return r * peers + owner - (r // whole_rounds) * (owner - owner // stride)

    def owns(r, owner):
        return (r // whole_rounds) * peers * lax.rem(owner, stride) + pair_of(r, owner) < pair_count

    def slab(t):
        return image_ref.at[t, :, pl.ds(start, width)]

    def forward(r, peer):
        return pltpu.make_async_remote_copy(
            src_ref=slab(pair_of(r, peer)), dst_ref=held.at[r, me],
            send_sem=sent.at[r, peer], recv_sem=landed.at[r, me],
            device_id=(group, peer), device_id_type=MESH)

    def forward_own(r):
        return pltpu.make_async_copy(slab(pair_of(r, me)), held.at[r, me], landed.at[r, me])

    def arrival(r, peer):
        return pltpu.make_async_remote_copy(
            src_ref=made.at[r, peer], dst_ref=held.at[r, peer],
            send_sem=sent.at[r, peer], recv_sem=landed.at[r, peer],
            device_id=(group, peer), device_id_type=MESH)

    def backward(r, peer):
        return pltpu.make_async_remote_copy(
            src_ref=made.at[r, peer], dst_ref=left_ref.at[pair_of(r, me)],
            send_sem=back_sent.at[r, peer], recv_sem=back_landed.at[r, me],
            device_id=(group, peer), device_id_type=MESH)

    def backward_own(r):
        return pltpu.make_async_copy(made.at[r, me], left_ref.at[pair_of(r, me)], back_landed.at[r, me])

    def back_arrival(r, peer):
        return pltpu.make_async_remote_copy(
            src_ref=made.at[r, peer], dst_ref=left_ref.at[pair_of(r, peer)],
            send_sem=back_sent.at[r, peer], recv_sem=back_landed.at[r, peer],
            device_id=(group, peer), device_id_type=MESH)

    def row_forward(i, peer):
        return pltpu.make_async_remote_copy(
            src_ref=rows_ref.at[peer * items + i], dst_ref=row_held.at[i, group],
            send_sem=row_sent.at[i, peer], recv_sem=row_landed.at[i, group],
            device_id=(peer, me), device_id_type=MESH)

    def row_forward_own(i):
        return pltpu.make_async_copy(
            rows_ref.at[group * items + i], row_held.at[i, group], row_landed.at[i, group])

    def row_arrival(i, peer):
        return pltpu.make_async_remote_copy(
            src_ref=rows_ref.at[peer * items + i], dst_ref=row_held.at[i, peer],
            send_sem=row_sent.at[i, peer], recv_sem=row_landed.at[i, peer],
            device_id=(peer, me), device_id_type=MESH)

    def row_backward(i, peer):
        return pltpu.make_async_remote_copy(
            src_ref=row_made.at[i, peer], dst_ref=back_ref.at[group * items + i],
            send_sem=row_back_sent.at[i, peer], recv_sem=row_back_landed.at[i, group],
            device_id=(peer, me), device_id_type=MESH)

    def row_backward_own(i):
        return pltpu.make_async_copy(
            row_made.at[i, group], back_ref.at[group * items + i], row_back_landed.at[i, group])

    def row_back_arrival(i, peer):
        return pltpu.make_async_remote_copy(
            src_ref=row_made.at[i, peer], dst_ref=back_ref.at[peer * items + i],
            send_sem=row_back_sent.at[i, peer], recv_sem=row_back_landed.at[i, peer],
            device_id=(peer, me), device_id_type=MESH)

    if first:
        early_width = early_ref.shape[2]
        early_columns = pl.ds(kept_ref.shape[3] - early_width, early_width)

        def early(i, peer):
            return pltpu.make_async_remote_copy(
                src_ref=kept_ref.at[i, peer, :, early_columns], dst_ref=early_ref.at[group * items + i],
                send_sem=early_sent.at[i, peer], recv_sem=early_landed.at[i, group],
                device_id=(peer, me), device_id_type=MESH)

        def early_own(i):
            return pltpu.make_async_copy(
                kept_ref.at[i, group, :, early_columns], early_ref.at[group * items + i],
                early_landed.at[i, group])

        def early_arrival(i, peer):
            return pltpu.make_async_remote_copy(
                src_ref=kept_ref.at[i, peer, :, early_columns], dst_ref=early_ref.at[peer * items + i],
                send_sem=early_sent.at[i, peer], recv_sem=early_landed.at[i, peer],
                device_id=(peer, me), device_id_type=MESH)

    def launch(r):
        for step in range(peers):
            peer = lax.rem(me + step, peers)

            @pl.when(owns(r, peer))
            def _(step=step, peer=peer):
                if step == 0:
                    forward_own(r).start()
                else:
                    forward(r, peer).start()

        def launch_row(i, carry):
            row_forward_own(i).start()
            for step in range(1, groups):
                row_forward(i, lax.rem(group + step, groups)).start()
            return carry

        lax.fori_loop(jnp.minimum(r * per_step, items), jnp.minimum((r + 1) * per_step, items), launch_row, 0)

    def ahead(r, carry):
        launch(r)
        return carry

    lax.fori_loop(0, min(AHEAD, rounds), ahead, 0)

    def mix(matrix_ref, i):
        total = jnp.dot(matrix_ref[0], row_held[i, 0], preferred_element_type=jnp.float32)
        for q in range(1, groups):
            total += jnp.dot(matrix_ref[q], row_held[i, q], preferred_element_type=jnp.float32)
        return total.reshape(groups, -1, total.shape[1])[:, :row_held.shape[2]]

    def mix_row(i, carry):
        row_forward_own(i).wait()
        for step in range(1, groups):
            row_arrival(i, lax.rem(group + step, groups)).wait_recv()
        weighted = mix(metric_ref, i)
        if first:
            half = weighted.astype(jnp.bfloat16)
            row_made[i] = half
            active = mix(active_ref, i) - shift_ref[0] * (weighted - half.astype(jnp.float32))
            kept_ref[i] = active.astype(jnp.bfloat16)
            early_own(i).start()
            for step in range(1, groups):
                early(i, lax.rem(group + step, groups)).start()
        else:
            wide, part = row_held.shape[3], row_made.shape[3]
            kept = kept_ref[i, :, :, :wide].astype(jnp.float32)
            row_made[i, :, :, :wide] = (kept + weighted).astype(jnp.bfloat16)
            if part > wide:
                row_made[i, :, :, wide:] = kept_ref[i, :, :, wide:part]
        row_backward_own(i).start()
        for step in range(1, groups):
            row_backward(i, lax.rem(group + step, groups)).start()
        return carry

    def body(r, carry):
        @pl.when(r + AHEAD < rounds)
        def _():
            launch(r + AHEAD)

        lax.fori_loop(jnp.minimum(r * per_step, items), jnp.minimum((r + 1) * per_step, items), mix_row, 0)

        @pl.when(owns(r, me))
        def _():
            forward_own(r).wait()
            for step in range(1, peers):
                arrival(r, lax.rem(me + step, peers)).wait_recv()
            block = held[r].reshape(peers * rows, width)
            product = jnp.dot(fock_ref[...], block, preferred_element_type=jnp.float32)
            made[r] = product.astype(jnp.bfloat16).reshape(peers, rows, width)
            backward_own(r).start()
            for step in range(1, peers):
                backward(r, lax.rem(me + step, peers)).start()

        return carry

    lax.fori_loop(0, rounds, body, 0)

    def drain(r, carry):
        mine = owns(r, me)

        @pl.when(mine)
        def _():
            backward_own(r).wait()

        for step in range(1, peers):
            peer = lax.rem(me + step, peers)

            @pl.when(owns(r, peer))
            def _(peer=peer):
                forward(r, peer).wait_send()
                back_arrival(r, peer).wait_recv()

            @pl.when(mine)
            def _(peer=peer):
                backward(r, peer).wait_send()

        return carry

    lax.fori_loop(0, rounds, drain, 0)

    def drain_row(i, carry):
        row_backward_own(i).wait()
        for step in range(1, groups):
            peer = lax.rem(group + step, groups)
            row_forward(i, peer).wait_send()
            row_back_arrival(i, peer).wait_recv()
            row_backward(i, peer).wait_send()
            if first:
                early_arrival(i, peer).wait_recv()
                early(i, peer).wait_send()
        if first:
            early_own(i).wait()
        return carry

    lax.fori_loop(0, items, drain_row, 0)


def stage(first, peers, groups, pairs, start, width, tail, smalls, kept, image, turned):
    fock = smalls[1] if first else smalls[0]
    padded = image.shape[1]
    count, tall, row_width = turned.shape
    items = count // groups
    rounds = -(-pairs // peers)
    full = image.shape[2]
    whole = pl.BlockSpec(memory_space=pltpu.VMEM)
    anywhere = pl.BlockSpec(memory_space=pl.ANY)
    kept_rows = (items, groups, tall, full)
    made_width = full if first else full - tail
    out_shape = [
        jax.ShapeDtypeStruct((pairs, padded, width), jnp.bfloat16),
        jax.ShapeDtypeStruct((count, tall, made_width), jnp.bfloat16),
    ]
    out_specs = [anywhere, anywhere]
    if first:
        in_specs = [pl.BlockSpec(memory_space=pltpu.SMEM)] + [whole] * 3
        out_shape.append(jax.ShapeDtypeStruct(kept_rows, jnp.bfloat16))
        out_shape.append(jax.ShapeDtypeStruct((count, tall, tail), jnp.bfloat16))
        out_specs += [whole, anywhere]
        operands = smalls
    else:
        in_specs = [whole] * 3
        operands = (*smalls, kept)
    dma = pltpu.SemaphoreType.DMA
    return pl.pallas_call(
        functools.partial(stage_kernel, first, peers, groups, pairs, start),
        out_shape=out_shape,
        in_specs=in_specs + [anywhere] * 2,
        out_specs=out_specs,
        scratch_shapes=[
            pltpu.VMEM((rounds, peers, padded, width), jnp.bfloat16),
            pltpu.VMEM((rounds, peers, padded, width), jnp.bfloat16),
            pltpu.VMEM((items, groups, tall, row_width), jnp.bfloat16),
            pltpu.VMEM((items, groups, tall, made_width), jnp.bfloat16),
            dma((rounds, peers)), dma((rounds, peers)), dma((rounds, peers)), dma((rounds, peers)),
            dma((items, groups)), dma((items, groups)), dma((items, groups)), dma((items, groups)),
        ] + [dma((items, groups))] * (2 if first else 0),
        compiler_params=pltpu.CompilerParams(
            collective_id=1 if first else 2, has_side_effects=True, vmem_limit_bytes=60 * 2**20),
        cost_estimate=pl.CostEstimate(
            flops=2 * pairs * fock.size * width, bytes_accessed=400 * 2**20, transcendentals=0),
    )(*operands, image, turned)


def finish_kernel(groups, peers, fock_ref, trial_ref, image_ref, left_ref, rest_ref, early_ref, out_ref, stats_ref,
                  trial, image, left, rest, sigma, part, slots, loaded, stored, sent, landed):
    group, me = lax.axis_index("act"), lax.axis_index("virt")
    count = groups * peers
    mine = group * peers + me
    barrier = pltpu.get_barrier_semaphore()
    chunks = loaded.shape[1]
    depth = trial.shape[0] // chunks
    rows, width = trial.shape[1], trial.shape[2]
    tail = left.shape[2]
    cut = width - tail

    def span(c):
        return pl.ds(c * depth, depth)

    def load(c, which):
        source, target = ((trial_ref, trial), (image_ref, image), (left_ref, left))[which]
        return pltpu.make_async_copy(source.at[span(c)], target.at[span(c)], loaded.at[which, c])

    def load_rest(c):
        head = rest_ref.shape[2]
        return (
            pltpu.make_async_copy(
                rest_ref.at[span(c)], rest.at[span(c), :, pl.ds(0, head)], loaded.at[3, c]),
            pltpu.make_async_copy(
                early_ref.at[span(c)], rest.at[span(c), :, pl.ds(head, width - head)], loaded.at[4, c]))

    def load_all(c, carry):
        for which in range(3):
            load(c, which).start()
        for copy in load_rest(c):
            copy.start()
        return carry

    lax.fori_loop(0, chunks, load_all, 0)

    def target(step):
        other = lax.rem(mine + step, count)
        return other, (other // peers, lax.rem(other, peers))

    def greet(step, carry):
        pl.semaphore_signal(barrier, inc=1, device_id=target(step)[1], device_id_type=MESH)
        return carry

    lax.fori_loop(1, count, greet, 0)

    def product(c, carry):
        numer, denom = carry
        for which in range(3):
            load(c, which).wait()
        for copy in load_rest(c):
            copy.wait()
        own = image[span(c)].reshape(depth * rows, width)
        total = jnp.dot(own, fock_ref[...], preferred_element_type=jnp.float32)
        total += rest[span(c)].reshape(depth * rows, width).astype(jnp.float32)
        last = total[:, cut:] + left[span(c)].reshape(depth * rows, tail).astype(jnp.float32)
        total = jnp.concatenate([total[:, :cut], last], axis=1)
        sigma[span(c)] = total.reshape(depth, rows, width)
        wide = trial[span(c)].reshape(depth * rows, width).astype(jnp.float32)
        numer += jnp.sum(wide * total, axis=0, keepdims=True)
        denom += jnp.sum(wide * own.astype(jnp.float32), axis=0, keepdims=True)
        return numer, denom

    zero = jnp.zeros((1, width), jnp.float32)
    numer, denom = lax.fori_loop(0, chunks, product, (zero, zero))
    pl.semaphore_wait(barrier, count - 1)

    def sum_all(phase, value):
        part[phase] = value

        def copy(step, slot):
            other, place = target(step)
            return pltpu.make_async_remote_copy(
                src_ref=part.at[phase], dst_ref=slots.at[phase, slot],
                send_sem=sent.at[phase, other], recv_sem=landed.at[phase, slot],
                device_id=place, device_id_type=MESH)

        def send(step, carry):
            copy(step, mine).start()
            return carry

        lax.fori_loop(1, count, send, 0)
        slots[phase, mine] = value

        def receive(step, carry):
            copy(step, target(step)[0]).wait_recv()
            return carry

        lax.fori_loop(1, count, receive, 0)

        def finish(step, carry):
            copy(step, mine).wait_send()
            return carry

        lax.fori_loop(1, count, finish, 0)
        return jnp.sum(slots[phase], axis=0)

    row = lax.broadcasted_iota(jnp.int32, (8, 128), 0)
    numer_one = jnp.sum(numer, axis=1, keepdims=True)
    denom_one = jnp.sum(denom, axis=1, keepdims=True)
    sums = sum_all(0, jnp.where(row == 0, numer_one, denom_one))
    denominator = sums[1:2, 0:1]
    rayleigh = sums[0:1, 0:1] / denominator

    def store(c):
        return pltpu.make_async_copy(rest.at[span(c)], out_ref.at[span(c)], stored.at[c])

    def residual(c, squares):
        own = image[span(c)].reshape(depth * rows, width).astype(jnp.float32)
        resid = sigma[span(c)].reshape(depth * rows, width) - rayleigh * own
        rest[span(c)] = resid.astype(jnp.bfloat16).reshape(depth, rows, width)
        store(c).start()
        return squares + jnp.sum(resid * resid, axis=0, keepdims=True)

    squares = lax.fori_loop(0, chunks, residual, zero)
    square_one = jnp.sum(squares, axis=1, keepdims=True)
    norms = sum_all(1, jnp.broadcast_to(square_one, (8, 128)))
    stats_ref[...] = jnp.where(row == 0, rayleigh, norms / denominator)

    def drain(c, carry):
        store(c).wait()
        return carry

    lax.fori_loop(0, chunks, drain, 0)


def finish(groups, peers, fock, trial, image, left, rest, early):
    pairs, rows, width = trial.shape
    depth = next(d for d in (5, 4, 2, 1) if pairs % d == 0)
    chunks = pairs // depth
    whole = pl.BlockSpec(memory_space=pltpu.VMEM)
    anywhere = pl.BlockSpec(memory_space=pl.ANY)
    dma = pltpu.SemaphoreType.DMA
    count = groups * peers
    return pl.pallas_call(
        functools.partial(finish_kernel, groups, peers),
        out_shape=[
            jax.ShapeDtypeStruct((pairs, rows, width), jnp.bfloat16),
            jax.ShapeDtypeStruct((8, 128), jnp.float32),
        ],
        in_specs=[whole] + [anywhere] * 5,
        out_specs=[anywhere, whole],
        scratch_shapes=[
            pltpu.VMEM((pairs, rows, width), jnp.bfloat16),
            pltpu.VMEM((pairs, rows, width), jnp.bfloat16),
            pltpu.VMEM((pairs, rows, left.shape[2]), jnp.bfloat16),
            pltpu.VMEM((pairs, rows, width), jnp.bfloat16),
            pltpu.VMEM((pairs, rows, width), jnp.float32),
            pltpu.VMEM((2, 8, 128), jnp.float32),
            pltpu.VMEM((2, count, 8, 128), jnp.float32),
            dma((5, chunks)), dma((chunks,)), dma((2, count)), dma((2, count)),
        ],
        compiler_params=pltpu.CompilerParams(
            collective_id=3, has_side_effects=True, vmem_limit_bytes=63 * 2**20),
    )(fock, trial, image, left, rest, early)


def local(amplitudes, virtual_fock_block, metric, active_block):
    pairs, rows, width = amplitudes.shape
    peers, groups = lax.axis_size("virt"), lax.axis_size("act")
    fock = virtual_fock_block
    padded = -(-rows // 16) * 16
    room = -pairs % 8
    cut = (3 * width // 5) // 128 * 128

    def widen(array):
        if padded == rows:
            return array
        return jnp.pad(array, ((0, 0), (0, padded - rows), (0, 0)))

    def turn(array):
        return jnp.transpose(array, (1, 0, 2))

    def turn_back(array):
        return jnp.transpose(array, (1, 0, 2))

    def pair_matrix(array):
        spread = jnp.pad(array.reshape(groups, pairs, groups, pairs), ((0, 0), (0, room), (0, 0), (0, 0)))
        return jnp.transpose(spread, (2, 0, 1, 3)).reshape(groups, groups * (pairs + room), pairs)

    spread = fock
    if padded != rows:
        gap = padded - rows
        spread = jnp.pad(
            fock.reshape(peers, rows, peers, rows), ((0, 0), (0, gap), (0, 0), (0, gap))
        ).reshape(peers * padded, peers * padded)
    metric_parts, active_parts = pair_matrix(metric), pair_matrix(active_block)
    at = lax.broadcasted_iota(jnp.int32, fock.shape, 0)
    across = lax.broadcasted_iota(jnp.int32, fock.shape, 1)
    shift = (2.0 / width) * jnp.sum(jnp.where(at == across, fock.astype(jnp.float32), 0.0))
    trial = widen(amplitudes)
    tail = min(128, width - cut)
    applied, weighted_turned, kept, early_turned = stage(
        True, peers, groups, pairs, 0, cut, tail, (shift.reshape(1), spread, metric_parts, active_parts),
        None, trial, turn(amplitudes))
    weighted = widen(turn_back(weighted_turned))
    left, rest_turned = stage(
        False, peers, groups, pairs, cut, width - cut, tail, (spread, metric_parts),
        kept, weighted, turn(applied[:, :rows]))
    rest = widen(turn_back(rest_turned))
    early = widen(turn_back(early_turned))
    resid, stats = finish(groups, peers, fock, trial, weighted, left, rest, early)
    return resid[:, :rows], stats[0, 0], stats[1, 0]


def solution(mesh):
    placed = (P("act", "virt", None), P(), P(), P())
    return jax.shard_map(
        local,
        mesh=mesh,
        in_specs=placed,
        out_specs=(P("act", "virt", None), P(), P()),
        check_vma=False,
    )
```

profile of v0, /device:TPU:1, one launch (start us, length us, event | category | flops | bytes accessed | tf_op | source)
XLA Modules:
  0.0 252.1 jit_solution(14866023623805847225)
XLA Ops:
  0.6 14.8 %reshape.28 = bf16[32,20,32,20]{3,2,1,0:T(8,128)(2,1)} reshape(bf16[640,640]{1,0:T(8,128)(2,1)} %fock_ref.1) | data formatting | bytes 1638400 | tf_op jit(solution)/shard_map/reshape | solution.py:482
  15.4 7.8 %pad.27 = bf16[32,32,32,32]{3,2,1,0:T(8,128)(2,1)} pad(bf16[32,20,32,20]{3,2,1,0:T(8,128)(2,1)} %reshape.28, bf16[]{:T(256)} %constant.1.clone.1), padding=0_0x0_12x0_0x0_12 | pad | bytes 2916354 | tf_op jit(solution)/shard_map/jit(_pad)/pad | solution.py:481
  23.2 0.0 copy-start.1
  23.2 12.6 %reshape.29.refs_1_.refs_0_ = bf16[1024,1024]{1,0:T(8,128)(2,1)} reshape(bf16[32,32,32,32]{3,2,1,0:T(8,128)(2,1)} %pad.27) | data formatting | bytes 4194304 | tf_op jit(solution)/shard_map/reshape | solution.py:483
  35.8 0.0 copy-done.1
  35.8 0.4 copy.15
  36.2 0.0 copy-start.4
  36.2 2.3 pad.26.refs_4_.trial_ref
  38.6 0.0 copy-done.4
  38.6 0.0 copy-start.5
  38.6 0.0 copy-start
  38.6 0.3 reshape.30
  38.8 0.1 copy.16
  38.9 0.9 pad.28
  39.8 0.0 copy-done.5
  39.8 0.3 reshape.32
  40.1 0.1 copy.17
  40.1 0.9 pad.29
  41.0 0.0 copy-done
  41.0 0.7 select_reduce_fusion
  42.3 88.1 %shard_map.67 = (bf16[100,32,384]{2,1,0:T(8,128)(2,1)}, bf16[20,100,640]{2,1,0:T(8,128)(2,1)}, bf16[5,4,100,640]{3,2,1,0:T(8,128)(2,1)}, bf16[20,100,128]{2,1,0:T(8,128)(2,1)}) custom-call(f32[1]{0:T(128)} %bitcast.refs_0_, bf16[1024,1024]{1,0:T(8,128)(2,1)} %reshape.29.refs_1_.refs_0_, bf16[4,416,100]{2,1,0:T(8,128)(2,1)} %bitcast.27, ...), custom_call_target="tpu_custom_call" | custom-call | flops 80530636800 | bytes 419430400 | tf_op jit(solution)/shard_map/pallas_call | solution.py:278
  130.5 2.2 copy.26
  132.7 0.0 copy-start.2
  132.7 2.4 pad.30.refs_3_.image_ref
  135.0 0.1 copy-done.2
  135.1 0.9 copy.19
  136.0 1.3 slice_bitcast_fusion.refs_4_
  137.3 54.7 %shard_map.68 = (bf16[100,32,256]{2,1,0:T(8,128)(2,1)}, bf16[20,100,512]{2,1,0:T(8,128)(2,1)}) custom-call(bf16[1024,1024]{1,0:T(8,128)(2,1)} %reshape.29.refs_1_.refs_0_, bf16[4,416,100]{2,1,0:T(8,128)(2,1)} %bitcast.28, bf16[5,4,100,640]{3,2,1,0:T(8,128)(2,1)} %get-tuple-element.12.refs_2_, bf16[100,32,640]{2,1,0:T(8,128)(2,1)} %pad.30.refs_3_.image_ref, ...), custom_call_target="tpu_custom_call" | custom-call | flops 53687091200 | bytes 419430400 | tf_op jit(solution)/shard_map/pallas_call | solution.py:278
  192.0 2.3 copy.27
  194.3 0.0 copy-start.3
  194.4 2.2 pad.31.rest_ref
  196.6 0.0 copy-done.3
  196.6 0.1 copy.28
  196.7 1.0 pad.32.early_ref
  197.7 49.1 %shard_map.69 = (bf16[100,32,640]{2,1,0:T(8,128)(2,1)}, f32[8,128]{1,0:T(8,128)}) custom-call(bf16[640,640]{1,0:T(8,128)(2,1)} %fock_ref.1, bf16[100,32,640]{2,1,0:T(8,128)(2,1)} %pad.26.refs_4_.trial_ref, bf16[100,32,640]{2,1,0:T(8,128)(2,1)} %pad.30.refs_3_.image_ref, bf16[100,32,256]{2,1,0:T(8,128)(2,1)} %get-tuple-element.14.left_ref, ...), custom_call_target="tpu_custom_call" | custom-call | tf_op jit(solution)/shard_map/pallas_call | solution.py:432
  246.8 2.1 slice.13
  249.0 1.8 copy.22
  250.8 1.3 fusion
Async XLA Ops:
  23.2 12.6 %copy-start.1 = (bf16[100,20,640]{2,0,1:T(8,128)(2,1)S(1)}, bf16[100,20,640]{2,0,1:T(8,128)(2,1)}, u32[]{:S(2)}) copy-start(bf16[100,20,640]{2,0,1:T(8,128)(2,1)} %param.4) | copy-start | bytes 7680004
  36.2 2.3 copy-start.4
  38.6 1.2 copy-start.5
  38.6 2.4 copy-start
  132.7 2.5 copy-start.2
  194.3 2.2 copy-start.3
where the time goes:
time: 253 us; the launch traced here: 252 us
  Pallas kernels  192 us (76%)
  local copies, waits for them, and re-layouts  58 us (23%)
    pallas_call x2, Pallas kernels, stage(): pl.pallas_call(functools.partial(stage_kernel, first, peers, groups, pair...  143 us
    pallas_call x1, Pallas kernels, finish(): pl.pallas_call(functools.partial(finish_kernel, groups, peers), out_shape...  49.1 us
    reshape x1, local copies, waits for them, and re-layouts, local(): fock.reshape(peers, rows, peers, rows)  14.8 us
    reshape x1, local copies, waits for them, and re-layouts, local(): spread = jnp.pad(fock.reshape(peers, rows, peers, rows), ((0, 0), (0, gap...  12.6 us
    pad x4, local copies, waits for them, and re-layouts, widen(): return jnp.pad(array, ((0, 0), (0, padded - rows), (0, 0)))  7.87 us
    pad x1, local copies, waits for them, and re-layouts, local(): jnp.pad(fock.reshape(peers, rows, peers, rows), ((0, 0), (0, gap), (0, 0)...  7.83 us
    pallas_call x4, local copies, waits for them, and re-layouts, stage(): pl.pallas_call(functools.partial(stage_kernel, first, peers, groups, pair...  5.45 us

commit v1 on v0

v1 whole, which is shorter than its diff:
```python
import functools

import jax
import jax.numpy as jnp
from jax import lax
from jax.experimental import pallas as pl
from jax.experimental.pallas import tpu as pltpu
from jax.sharding import PartitionSpec as P

MESH = pl.DeviceIdType.MESH
LANES = 128
F32, BF16 = jnp.float32, jnp.bfloat16


def round_up(value, unit):
    return -(-value // unit) * unit


def one_hot(shape, place, axis, every, gap):
    index = lax.broadcasted_iota(jnp.int32, shape, axis)
    other = lax.broadcasted_iota(jnp.int32, shape, 1 - axis)
    return jnp.where(index + gap * (index // every) + place == other, 1.0, 0.0).astype(BF16)


def sigma_kernel(groups, peers, x_ref, fock_ref, metric_ref, active_ref, out_ref, stats_ref,
                 trial, fock, metric, active, spread, mats, gathered, surplus, leaving, local, coming,
                 trial_wide, image_wide, image, held, made, back, sigma, row_sums, sum_slots,
                 loaded, small_loaded, row_sent, row_landed, field_sent, field_landed,
                 sent, landed, spare_sent, spare_landed,
                 back_sent, back_landed, back_spare_sent, back_spare_landed,
                 stored, sum_sent, sum_landed):
    group, me = lax.axis_index("act"), lax.axis_index("virt")
    chunks, pairs, tall = trial.shape[0], trial.shape[1], trial.shape[2]
    rows = x_ref.shape[1]
    width = x_ref.shape[2]
    high = gathered.shape[4]
    part = rows // groups
    share, spares = pairs // peers, pairs % peers
    stride = peers // spares
    right, left = lax.rem(group + 1, groups), lax.rem(group + groups - 1, groups)
    opposite = lax.rem(group + 2, groups)
    real = pl.ds(0, rows)
    real_pairs = pl.ds(0, pairs)

    def load(c):
        return pltpu.make_async_copy(
            x_ref.at[:, :, pl.ds(pl.multiple_of(c * LANES, LANES), LANES)], trial.at[c, :, real], loaded.at[c])

    smalls = [pltpu.make_async_copy(source, target, small_loaded.at[i]) for i, (source, target) in enumerate(
        ((metric_ref, metric), (active_ref, active), (fock_ref, fock)))]
    for c in range(chunks):
        load(c).start()
    for copy in smalls:
        copy.start()

    extra = pl.ds(rows, tall - rows)
    zero_rows = tall - rows

    def clear(c, carry):
        held[c, :, :, extra] = jnp.zeros(held.shape[1:3] + (zero_rows, LANES), BF16)
        back[c, :, extra] = jnp.zeros((pairs, zero_rows, LANES), BF16)
        trial[c, :, extra] = jnp.zeros((pairs, zero_rows, LANES), BF16)
        for q in range(zero_rows):
            sigma[c, pl.ds(rows + q, high, stride=tall)] = jnp.zeros((high, LANES), F32)
        gathered[c, :, :, :, pl.ds(pairs, high - pairs)] = jnp.zeros(
            gathered.shape[1:4] + (high - pairs, LANES), BF16)
        return carry

    lax.fori_loop(0, chunks, clear, 0)
    trial_wide[pl.ds(pairs * tall, (high - pairs) * tall)] = jnp.zeros(((high - pairs) * tall, LANES), F32)
    for q in range(zero_rows):
        image_wide[pl.ds(rows + q, high, stride=tall)] = jnp.zeros((high, LANES), F32)

    barrier = pltpu.get_barrier_semaphore()

    def greet(step, carry):
        pl.semaphore_signal(barrier, inc=1, device_id=(group, lax.rem(me + step, peers)), device_id_type=MESH)
        return carry

    lax.fori_loop(1, peers, greet, 0)
    for step in range(1, groups):
        pl.semaphore_signal(barrier, inc=1, device_id=(lax.rem(group + step, groups), me), device_id_type=MESH)
    pl.semaphore_wait(barrier, peers + groups - 2)

    def row_copy(c, which, source, kind, owner, target):
        return pltpu.make_async_remote_copy(
            src_ref=source.at[:, real_pairs], dst_ref=gathered.at[c, kind, owner, :, real_pairs],
            send_sem=row_sent.at[c, which], recv_sem=row_landed.at[c, kind, owner],
            device_id=(target, me), device_id_type=MESH)

    def row_sends(c):
        return (
            row_copy(c, 0, surplus.at[c, 0], 0, group, right),
            row_copy(c, 1, surplus.at[c, 1], 1, group, left),
            row_copy(c, 2, gathered.at[c, 0, group], 1, group, right),
            row_copy(c, 3, gathered.at[c, 1, group], 0, group, left))

    def row_forwards(c):
        return (
            row_copy(c, 4, gathered.at[c, 0, left], 1, left, right),
            row_copy(c, 5, gathered.at[c, 1, right], 0, right, left))

    def row_arrival(c, kind, owner):
        return row_copy(c, 0, surplus.at[c, 0], kind, owner, right)

    def field_copy(c, kind):
        return pltpu.make_async_remote_copy(
            src_ref=leaving.at[c, kind, :, :, real_pairs], dst_ref=coming.at[c, kind, :, :, real_pairs],
            send_sem=field_sent.at[c, kind], recv_sem=field_landed.at[c, kind],
            device_id=((left, right)[kind], me), device_id_type=MESH)

    def spare_place(c):
        return lax.rem(2 * c + c // 4, stride)

    def peer_at(step):
        return lax.rem(me + step, peers)

    def forward(c, peer):
        return pltpu.make_async_remote_copy(
            src_ref=image.at[c, pl.ds(peer * share, share), real],
            dst_ref=held.at[c, pl.ds(0, share), me, real],
            send_sem=sent.at[c, peer], recv_sem=landed.at[c, me],
            device_id=(group, peer), device_id_type=MESH)

    def arrival(c, peer):
        return pltpu.make_async_remote_copy(
            src_ref=image.at[c, pl.ds(peer * share, share), real],
            dst_ref=held.at[c, pl.ds(0, share), peer, real],
            send_sem=sent.at[c, peer], recv_sem=landed.at[c, peer],
            device_id=(group, peer), device_id_type=MESH)

    def spare_forward(c, j, peer):
        return pltpu.make_async_remote_copy(
            src_ref=image.at[c, share * peers + j, real], dst_ref=held.at[c, share, me, real],
            send_sem=spare_sent.at[c, j], recv_sem=spare_landed.at[c, me],
            device_id=(group, peer), device_id_type=MESH)

    def spare_arrival(c, peer):
        return pltpu.make_async_remote_copy(
            src_ref=image.at[c, share * peers, real], dst_ref=held.at[c, share, peer, real],
            send_sem=spare_sent.at[c, 0], recv_sem=spare_landed.at[c, peer],
            device_id=(group, peer), device_id_type=MESH)

    def backward(c, peer):
        return pltpu.make_async_remote_copy(
            src_ref=made.at[c, pl.ds(0, share), peer, real],
            dst_ref=back.at[c, pl.ds(me * share, share), real],
            send_sem=back_sent.at[c, peer], recv_sem=back_landed.at[c, me],
            device_id=(group, peer), device_id_type=MESH)

    def back_arrival(c, peer):
        return pltpu.make_async_remote_copy(
            src_ref=made.at[c, pl.ds(0, share), peer, real],
            dst_ref=back.at[c, pl.ds(peer * share, share), real],
            send_sem=back_sent.at[c, peer], recv_sem=back_landed.at[c, peer],
            device_id=(group, peer), device_id_type=MESH)

    def spare_backward(c, peer):
        return pltpu.make_async_remote_copy(
            src_ref=made.at[c, share, peer, real],
            dst_ref=back.at[c, share * peers + me // stride, real],
            send_sem=back_spare_sent.at[c, peer], recv_sem=back_spare_landed.at[c, me // stride],
            device_id=(group, peer), device_id_type=MESH)

    def spare_back_arrival(c, j, peer):
        return pltpu.make_async_remote_copy(
            src_ref=made.at[c, share, peer, real], dst_ref=back.at[c, share * peers + j, real],
            send_sem=back_spare_sent.at[c, peer], recv_sem=back_spare_landed.at[c, j],
            device_id=(group, peer), device_id_type=MESH)

    def owns_spare(c):
        return lax.rem(me, stride) == spare_place(c)

    def send_rows(c):
        load(c).wait()

        def widen(b, carry):
            trial_wide[pl.ds(pl.multiple_of(b * 10 * tall, 8), 10 * tall)] = trial[
                c, pl.ds(b * 10, 10)].astype(F32).reshape(10 * tall, LANES)
            return carry

        lax.fori_loop(0, pairs // 10, widen, 0)
        for p in range(groups):
            first = lax.rem(group + p, groups) * part
            for j in range(part):
                turned = trial_wide[pl.ds(first + j, high, stride=tall)].astype(BF16)
                if p == 0:
                    gathered[c, 0, group, j] = turned
                elif p == groups - 1:
                    gathered[c, 1, group, j] = turned
                else:
                    surplus[c, p - 1, j] = turned
        for copy in row_sends(c):
            copy.start()

    def prepare():
        for copy in smalls:
            copy.wait()
        count = groups * pairs
        spread_pairs = one_hot((count, groups * high), 0, 0, pairs, high - pairs)
        for which, matrix in enumerate((metric, active)):
            wide = jnp.dot(matrix[...], spread_pairs, preferred_element_type=F32).astype(BF16)
            for kind in range(2):
                at = lax.broadcasted_iota(jnp.int32, (2 * high, count), 0)
                column = lax.broadcasted_iota(jnp.int32, (2 * high, count), 1)
                other = left if kind == 0 else right
                wanted = jnp.where(at < high, at + group * pairs, at - high + other * pairs)
                kept = jnp.where(at < high, at, at - high) < pairs
                choose = jnp.where((wanted == column) & kept, 1.0, 0.0).astype(BF16)
                mats[kind, pl.ds(2 * high * which, 2 * high)] = jnp.dot(
                    choose, wide, preferred_element_type=F32).astype(BF16)
        across = one_hot((width, peers * tall), 0, 0, rows, tall - rows)
        down = one_hot((peers * tall, width), 0, 1, rows, tall - rows)
        half = jnp.dot(fock[...], across, preferred_element_type=F32).astype(BF16)
        spread[...] = jnp.dot(down, half, preferred_element_type=F32).astype(BF16)

    def shift_of():
        at = lax.broadcasted_iota(jnp.int32, fock.shape, 0)
        column = lax.broadcasted_iota(jnp.int32, fock.shape, 1)
        diagonal = jnp.where(at == column, fock[...].astype(F32), 0.0)
        return (2.0 / width) * jnp.sum(jnp.sum(diagonal, axis=0, keepdims=True), axis=1, keepdims=True)

    def pass_rows(c):
        row_arrival(c, 0, left).wait_recv()
        row_arrival(c, 1, right).wait_recv()
        for copy in row_forwards(c):
            copy.start()

    def mix(c):
        shift = row_sums[0, 0:1, 0:1]
        row_arrival(c, 0, right).wait_recv()
        row_arrival(c, 1, left).wait_recv()
        row_arrival(c, 0, opposite).wait_recv()
        row_arrival(c, 1, opposite).wait_recv()
        for kind in range(2):
            block = jnp.concatenate(
                [gathered[c, kind, :, j].reshape(groups * high, LANES) for j in range(part)], axis=1)
            both = jnp.dot(mats[kind], block, preferred_element_type=F32)
            weighted = both[:2 * high]
            half = weighted.astype(BF16)
            rest = (both[2 * high:] - shift * (weighted - half.astype(F32))).astype(BF16)
            for field, value in enumerate((half, rest)):
                for j in range(part):
                    some = slice(LANES * j, LANES * (j + 1))
                    local[c, kind, field, j] = value[:high, some]
                    leaving[c, kind, field, j] = value[high:, some]
            field_copy(c, kind).start()

    def turn(c, source, quarter):
        first = quarter * part
        for j in range(part):
            image_wide[pl.ds(first + j, high, stride=tall)] = source[0, j].astype(F32)
            sigma[c, pl.ds(first + j, high, stride=tall)] = source[1, j].astype(F32)

    def send_image(c):
        turn(c, local.at[c, 0], group)
        turn(c, local.at[c, 1], left)
        field_copy(c, 0).wait_recv()
        turn(c, coming.at[c, 0], right)
        field_copy(c, 1).wait_recv()
        turn(c, coming.at[c, 1], opposite)

        def narrow(b, carry):
            image[c, pl.ds(b * 10, 10)] = image_wide[
                pl.ds(pl.multiple_of(b * 10 * tall, 8), 10 * tall)].astype(BF16).reshape(10, tall, LANES)
            return carry

        lax.fori_loop(0, pairs // 10, narrow, 0)

        def send(step, carry):
            forward(c, peer_at(step)).start()
            return carry

        lax.fori_loop(1, peers, send, 0)
        for j in range(spares):
            owner = stride * j + spare_place(c)

            @pl.when(owner != me)
            def _(j=j, owner=owner):
                spare_forward(c, j, owner).start()

            @pl.when(owner == me)
            def _(j=j):
                held[c, share, me] = image[c, share * peers + j]

        held[c, pl.ds(0, share), me] = image[c, pl.ds(me * share, share)]

    def apply_fock(c):
        def receive(step, carry):
            arrival(c, peer_at(step)).wait_recv()
            return carry

        lax.fori_loop(1, peers, receive, 0)
        block = jnp.concatenate([held[c, i].reshape(peers * tall, LANES) for i in range(share)], axis=1)
        product = jnp.dot(spread[...], block, preferred_element_type=F32).astype(BF16)
        for i in range(share):
            made[c, i] = product[:, LANES * i:LANES * (i + 1)].reshape(peers, tall, LANES)

        def send(step, carry):
            backward(c, peer_at(step)).start()
            return carry

        lax.fori_loop(1, peers, send, 0)
        back[c, pl.ds(me * share, share)] = made[c, pl.ds(0, share), me]

        @pl.when(owns_spare(c))
        def _():
            def receive_spare(step, carry):
                spare_arrival(c, peer_at(step)).wait_recv()
                return carry

            lax.fori_loop(1, peers, receive_spare, 0)
            one = jnp.dot(spread[...], held[c, share].reshape(peers * tall, LANES), preferred_element_type=F32)
            made[c, share] = one.astype(BF16).reshape(peers, tall, LANES)

            def send_spare(step, carry):
                spare_backward(c, peer_at(step)).start()
                return carry

            lax.fori_loop(1, peers, send_spare, 0)
            back[c, share * peers + me // stride] = made[c, share, me]

    def apply_right():
        def block(b, carry):
            own = jnp.concatenate(
                [image[c, pl.ds(b * 10, 10)].reshape(10 * tall, LANES) for c in range(chunks)], axis=1)
            product = jnp.dot(own, fock[...], preferred_element_type=F32)
            at = pl.ds(pl.multiple_of(b * 10 * tall, 8), 10 * tall)
            for c in range(chunks):
                sigma[c, at] += product[:, LANES * c:LANES * (c + 1)]
            return carry

        lax.fori_loop(0, pairs // 10, block, 0)

    def tick(n, carry):
        def stage(c, run):
            @pl.when((c >= 0) & (c < chunks))
            def _():
                run(c)

        stage(n + 1, pass_rows)
        stage(n, mix)
        stage(n + 3, send_rows)

        @pl.when(n == -2)
        def _():
            prepare()
            row_sums[0] = jnp.broadcast_to(shift_of(), (8, LANES))

        @pl.when(n == chunks + 1)
        def _():
            apply_right()

        stage(n - 2, apply_fock)
        stage(n - 1, send_image)
        return carry

    lax.fori_loop(-3, chunks + 2, tick, 0)

    shift = row_sums[0, 0:1, 0:1]
    zero = jnp.zeros((8, LANES), F32)

    def combine(c, sums):
        def receive(step, carry):
            back_arrival(c, peer_at(step)).wait_recv()
            return carry

        lax.fori_loop(1, peers, receive, 0)
        for j in range(spares):
            owner = stride * j + spare_place(c)

            @pl.when(owner != me)
            def _(j=j, owner=owner):
                spare_back_arrival(c, j, owner).wait_recv()

        def block(b, sums):
            at = pl.ds(pl.multiple_of(b * 10 * tall, 8), 10 * tall)
            some = pl.ds(b * 10, 10)
            x = trial[c, some].astype(F32).reshape(10 * tall, LANES)
            w = image[c, some].astype(F32).reshape(10 * tall, LANES)
            s = sigma[c, at] + back[c, some].astype(F32).reshape(10 * tall, LANES) - shift * w
            sigma[c, at] = s
            products = (x * s, x * w, s * s, s * w, w * w)
            return tuple(
                total + jnp.sum(term.reshape(10 * tall // 8, 8, LANES), axis=0)
                for total, term in zip(sums, products))

        return lax.fori_loop(0, pairs // 10, block, sums)

    sums = lax.fori_loop(0, chunks, combine, (zero,) * 5)
    lane = lax.broadcasted_iota(jnp.int32, (8, LANES), 1)
    packed = zero
    for q, total in enumerate(sums):
        one = jnp.sum(jnp.sum(total, axis=0, keepdims=True), axis=1, keepdims=True)
        packed = jnp.where(lane == q, one, packed)

    def sum_all(phase, value, count, place):
        row_sums[1 + phase] = value

        def copy(other, slot):
            return pltpu.make_async_remote_copy(
                src_ref=row_sums.at[1 + phase], dst_ref=sum_slots.at[phase, slot],
                send_sem=sum_sent.at[phase, other], recv_sem=sum_landed.at[phase, slot],
                device_id=place(other), device_id_type=MESH)

        mine = me if phase == 0 else group

        def send(step, carry):
            copy(lax.rem(mine + step, count), mine).start()
            return carry

        lax.fori_loop(1, count, send, 0)
        sum_slots[phase, mine] = value

        def receive(step, carry):
            other = lax.rem(mine + step, count)
            copy(other, other).wait()
            return carry

        lax.fori_loop(1, count, receive, 0)
        return jnp.sum(sum_slots[phase, pl.ds(0, count)], axis=0)

    packed = sum_all(0, packed, peers, lambda other: (group, other))
    packed = sum_all(1, packed, groups, lambda other: (other, me))
    numer, denom, ss, sw, ww = (packed[0:1, q:q + 1] for q in range(5))
    ratio = numer / denom
    norm = (ss - 2.0 * ratio * sw + ratio * ratio * ww) / denom
    stats_ref[...] = jnp.where(lane == 0, ratio + shift, norm)

    def store(c):
        return pltpu.make_async_copy(
            trial.at[c, :, real], out_ref.at[:, :, pl.ds(pl.multiple_of(c * LANES, LANES), LANES)], stored.at[c])

    def finish(c, carry):
        def block(b, carry):
            at = pl.ds(pl.multiple_of(b * 10 * tall, 8), 10 * tall)
            some = pl.ds(b * 10, 10)
            w = image[c, some].astype(F32).reshape(10 * tall, LANES)
            trial[c, some] = (sigma[c, at] - ratio * w).astype(BF16).reshape(10, tall, LANES)
            return carry

        lax.fori_loop(0, pairs // 10, block, 0)
        store(c).start()
        return carry

    lax.fori_loop(0, chunks, finish, 0)

    def drain(c, carry):
        for copy in row_sends(c) + row_forwards(c):
            copy.wait_send()
        for kind in range(2):
            field_copy(c, kind).wait_send()

        def sends(step, carry):
            forward(c, peer_at(step)).wait_send()
            backward(c, peer_at(step)).wait_send()
            return carry

        lax.fori_loop(1, peers, sends, 0)
        for j in range(spares):
            owner = stride * j + spare_place(c)

            @pl.when(owner != me)
            def _(j=j, owner=owner):
                spare_forward(c, j, owner).wait_send()

        @pl.when(owns_spare(c))
        def _():
            def spare_sends(step, carry):
                spare_backward(c, peer_at(step)).wait_send()
                return carry

            lax.fori_loop(1, peers, spare_sends, 0)

        store(c).wait()
        return carry

    lax.fori_loop(0, chunks, drain, 0)


def local(amplitudes, virtual_fock_block, metric, active_block):
    pairs, rows, width = amplitudes.shape
    peers, groups = lax.axis_size("virt"), lax.axis_size("act")
    chunks = width // LANES
    tall, high = round_up(rows, 8), round_up(pairs, 8)
    part = rows // groups
    items = pairs // peers + 1
    anywhere = pl.BlockSpec(memory_space=pl.ANY)
    dma = pltpu.SemaphoreType.DMA

    def half(*shape):
        return pltpu.VMEM(shape, BF16)

    def wide(*shape):
        return pltpu.VMEM(shape, F32)

    resid, stats = pl.pallas_call(
        functools.partial(sigma_kernel, groups, peers),
        out_shape=[
            jax.ShapeDtypeStruct(amplitudes.shape, BF16),
            jax.ShapeDtypeStruct((8, LANES), F32),
        ],
        in_specs=[anywhere] * 4,
        out_specs=[anywhere, pl.BlockSpec(memory_space=pltpu.VMEM)],
        scratch_shapes=[
            half(chunks, pairs, tall, LANES),
            half(*virtual_fock_block.shape), half(*metric.shape), half(*active_block.shape),
            half(peers * tall, peers * tall),
            half(2, groups * high, groups * high),
            half(chunks, 2, groups, part, high, LANES),
            half(chunks, 2, part, high, LANES),
            half(chunks, 2, 2, part, high, LANES),
            half(chunks, 2, 2, part, high, LANES),
            half(chunks, 2, 2, part, high, LANES),
            wide(high * tall, LANES), wide(high * tall, LANES),
            half(chunks, pairs, tall, LANES),
            half(chunks, items, peers, tall, LANES),
            half(chunks, items, peers, tall, LANES),
            half(chunks, pairs, tall, LANES),
            wide(chunks, high * tall, LANES),
            wide(3, 8, LANES),
            wide(2, peers, 8, LANES),
            dma((chunks,)), dma((3,)),
            dma((chunks, 6)), dma((chunks, 2, groups)),
            dma((chunks, 2)), dma((chunks, 2)),
            dma((chunks, peers)), dma((chunks, peers)), dma((chunks, 4)), dma((chunks, peers)),
            dma((chunks, peers)), dma((chunks, peers)), dma((chunks, peers)), dma((chunks, 4)),
            dma((chunks,)), dma((2, peers)), dma((2, peers)),
        ],
        compiler_params=pltpu.CompilerParams(
            collective_id=1, has_side_effects=True, vmem_limit_bytes=62 * 2**20),
    )(amplitudes, virtual_fock_block, metric, active_block)
    return resid, stats[0, 0], stats[0, 1]


def solution(mesh):
    return jax.shard_map(
        local,
        mesh=mesh,
        in_specs=(P("act", "virt", None), P(), P(), P()),
        out_specs=(P("act", "virt", None), P(), P()),
        check_vma=False,
    )
```

time: 253 us -> 158 us (0.62)
  local copies, waits for them, and re-layouts: 58 us -> 8.89 us
  Pallas kernels: 192 us -> 148 us
    pallas_call x3 -> x1, Pallas kernels: 192 us -> 148 us  [local(): pl.pallas_call(functools.partial(sigma_kernel, groups, peers), out_shape=...]
    reshape x6 -> x0, local copies, waits for them, and re-layouts: 28 us -> none  [the longest x1 14.8 us: local(): fock.reshape(peers, rows, peers, rows)]
    pad x7 -> x0, local copies, waits for them, and re-layouts: 17.4 us -> none  [the longest x4 7.87 us: widen(): return jnp.pad(array, ((0, 0), (0, padded - rows), (0, 0)))]
    pallas_call x4 -> x0, local copies, waits for them, and re-layouts: 5.45 us -> none  [stage(): pl.pallas_call(functools.partial(stage_kernel, first, peers, groups, pair...]
    unnamed x14 -> x2, local copies, waits for them, and re-layouts: 2.39 us -> 7.55 us
where the time goes in v1:
time: 158 us; the launch traced here: 157 us
  Pallas kernels  148 us (94%)
  local copies, waits for them, and re-layouts  8.89 us (6%)
    pallas_call x1, Pallas kernels, local(): pl.pallas_call(functools.partial(sigma_kernel, groups, peers), out_shape=...  148 us
    unnamed x2, local copies, waits for them, and re-layouts  7.55 us

profile of v1, /device:TPU:1, one launch (start us, length us, event | category | flops | bytes accessed | tf_op | source)
XLA Modules:
  0.0 157.3 jit_solution(2666312608012911308)
XLA Ops:
  0.6 3.8 %copy.7.x_ref = bf16[100,20,640]{2,1,0:T(8,128)(2,1)} copy(bf16[100,20,640]{2,0,1:T(8,128)(2,1)} %param.4) | data formatting | bytes 5120000 | tf_op args[0]
  4.5 147.8 %shard_map.67 = (bf16[100,20,640]{2,1,0:T(8,128)(2,1)}, f32[8,128]{1,0:T(8,128)}) custom-call(bf16[100,20,640]{2,1,0:T(8,128)(2,1)} %copy.7.x_ref, bf16[640,640]{1,0:T(8,128)(2,1)} %fock_ref.1, bf16[400,400]{1,0:T(8,128)(2,1)} %metric_ref.1, bf16[400,400]{1,0:T(8,128)(2,1)} %active_ref.1), custom_call_target="tpu_custom_call" | custom-call | tf_op jit(solution)/shard_map/pallas_call | solution.py:497
  152.3 3.7 %copy.8 = bf16[100,20,640]{2,0,1:T(8,128)(2,1)} copy(bf16[100,20,640]{2,1,0:T(8,128)(2,1)} %get-tuple-element.7) | data formatting | bytes 5120000
  156.0 1.3 fusion

commit v2 on v1

v2 whole, which is shorter than its diff:
```python
import functools

import jax
import jax.numpy as jnp
from jax import lax
from jax.experimental import pallas as pl
from jax.experimental.pallas import tpu as pltpu
from jax.sharding import PartitionSpec as P

MESH = pl.DeviceIdType.MESH
LANES = 128
F32, BF16 = jnp.float32, jnp.bfloat16


def round_up(value, unit):
    return -(-value // unit) * unit


def sigma_kernel(groups, peers, x_ref, fock_ref, metric_ref, active_ref, out_ref, stats_ref,
                 own, fock, metric, active, spread, mats, gathered, fields, leaving,
                 wide, image, held, made, back, sigma, row_sums, sum_slots,
                 loaded, small_loaded, row_sent, row_landed, field_sent, field_landed, active_landed,
                 sent, landed, spare_sent, spare_landed,
                 back_sent, back_landed, back_spare_sent, back_spare_landed,
                 stored, sum_sent, sum_landed):
    group, me = lax.axis_index("act"), lax.axis_index("virt")
    chunks, pairs, tall = image.shape[0], image.shape[1], image.shape[2]
    rows, width = x_ref.shape[0], x_ref.shape[2]
    part, high = own.shape[2], own.shape[3]
    share, spares = pairs // peers, pairs % peers
    stride = peers // spares
    right, left = lax.rem(group + 1, groups), lax.rem(group + groups - 1, groups)
    opposite = lax.rem(group + 2, groups)
    others = (right, left, opposite)
    RIGHT, LEFT, OPPOSITE = range(3)
    real = pl.ds(0, rows)
    real_pairs = pl.ds(0, pairs)
    depth = 10

    def quarter(p):
        return lax.rem(group + p, groups)

    def columns(c):
        return pl.ds(pl.multiple_of(c * LANES, LANES), LANES)

    def load(c, p):
        return pltpu.make_async_copy(
            x_ref.at[pl.ds(quarter(p) * part, part), :, columns(c)], own.at[c, p, :, real_pairs], loaded.at[c])

    smalls = [pltpu.make_async_copy(source, target, small_loaded.at[i]) for i, (source, target) in enumerate(
        ((metric_ref, metric), (active_ref, active), (fock_ref, fock)))]

    def start_loads(c, carry):
        for p in range(groups):
            load(c, p).start()
        return carry

    lax.fori_loop(0, chunks, start_loads, 0)
    for copy in smalls:
        copy.start()

    barrier = pltpu.get_barrier_semaphore()
    extra = pl.ds(rows, tall - rows)
    beyond = pl.ds(pairs, high - pairs)

    def clear(c, carry):
        held[c, :, :, extra] = jnp.zeros(held.shape[1:3] + (tall - rows, LANES), BF16)
        gathered[c, :, :, :, beyond] = jnp.zeros(gathered.shape[1:4] + (high - pairs, LANES), BF16)
        own[c, :, :, beyond] = jnp.zeros(own.shape[1:3] + (high - pairs, LANES), BF16)
        fields[c, :, :, :, beyond] = jnp.zeros(fields.shape[1:4] + (high - pairs, LANES), BF16)
        return carry

    lax.fori_loop(0, chunks, clear, 0)

    def greet(step, carry):
        pl.semaphore_signal(barrier, inc=1, device_id=(group, lax.rem(me + step, peers)), device_id_type=MESH)
        return carry

    lax.fori_loop(1, peers, greet, 0)
    for step in range(1, groups):
        pl.semaphore_signal(barrier, inc=1, device_id=(lax.rem(group + step, groups), me), device_id_type=MESH)
    for q in range(tall - rows):
        wide[pl.ds(rows + q, high, stride=tall)] = jnp.zeros((high, LANES), F32)
    pl.semaphore_wait(barrier, peers + groups - 2)

    def settle(ref, semaphore):
        pltpu.make_async_copy(ref, ref, semaphore).wait()

    def row_copy(c, wave, source, kind, slot, target):
        return pltpu.make_async_remote_copy(
            src_ref=source.at[:, real_pairs], dst_ref=gathered.at[c, kind, slot, :, real_pairs],
            send_sem=row_sent.at[c], recv_sem=row_landed.at[c, wave],
            device_id=(target, me), device_id_type=MESH)

    def early_rows(c):
        return row_copy(c, 0, own.at[c, 1], 0, LEFT, right), row_copy(c, 0, own.at[c, 2], 1, RIGHT, left)

    def late_rows(c):
        return row_copy(c, 1, own.at[c, 0], 1, LEFT, right), row_copy(c, 1, own.at[c, 3], 0, RIGHT, left)

    def row_forwards(c):
        return (
            row_copy(c, 2, gathered.at[c, 0, LEFT], 1, OPPOSITE, right),
            row_copy(c, 2, gathered.at[c, 1, RIGHT], 0, OPPOSITE, left))

    def settle_rows(c, wave):
        settle(gathered.at[c, 0, pl.ds(0, 2), :, real_pairs], row_landed.at[c, wave])

    def field_copy(c, field, kind):
        return pltpu.make_async_remote_copy(
            src_ref=leaving.at[c, kind, field, :, real_pairs], dst_ref=fields.at[c, 1 + kind, field, :, real_pairs],
            send_sem=field_sent.at[c], recv_sem=active_landed.at[c] if field else field_landed.at[c, kind],
            device_id=((left, right)[kind], me), device_id_type=MESH)

    def spare_place(c):
        return lax.rem(2 * c + c // 4, stride)

    def peer_at(step):
        return lax.rem(me + step, peers)

    def forward(c, peer):
        return pltpu.make_async_remote_copy(
            src_ref=image.at[c, pl.ds(peer * share, share), real],
            dst_ref=held.at[c, pl.ds(0, share), me, real],
            send_sem=sent.at[c], recv_sem=landed.at[c],
            device_id=(group, peer), device_id_type=MESH)

    def spare_forward(c, j, peer):
        return pltpu.make_async_remote_copy(
            src_ref=image.at[c, share * peers + j, real], dst_ref=held.at[c, share, me, real],
            send_sem=spare_sent.at[c], recv_sem=spare_landed.at[c],
            device_id=(group, peer), device_id_type=MESH)

    def backward(c, peer):
        return pltpu.make_async_remote_copy(
            src_ref=made.at[c, pl.ds(0, share), peer, real],
            dst_ref=back.at[c, pl.ds(me * share, share), real],
            send_sem=back_sent.at[c], recv_sem=back_landed.at[c],
            device_id=(group, peer), device_id_type=MESH)

    def spare_backward(c, peer):
        return pltpu.make_async_remote_copy(
            src_ref=made.at[c, share, peer, real],
            dst_ref=back.at[c, share * peers + me // stride, real],
            send_sem=back_spare_sent.at[c], recv_sem=back_spare_landed.at[c],
            device_id=(group, peer), device_id_type=MESH)

    def settle_spares(c, ref, semaphore):
        mine = owns_spare(c)

        @pl.when(mine)
        def _():
            settle(ref.at[c, pl.ds(0, spares - 1), real], semaphore.at[c])

        @pl.when(jnp.logical_not(mine))
        def _():
            settle(ref.at[c, pl.ds(0, spares), real], semaphore.at[c])

    def owns_spare(c):
        return lax.rem(me, stride) == spare_place(c)

    def send_early_rows(c):
        settle(own.at[c, :, :, real_pairs], loaded.at[c])
        for copy in early_rows(c):
            copy.start()

    def send_late_rows(c):
        for copy in late_rows(c):
            copy.start()

    def prepare_mix():
        for copy in smalls:
            copy.wait()
        count = groups * pairs
        at = lax.broadcasted_iota(jnp.int32, (count, groups * high), 1)
        line = lax.broadcasted_iota(jnp.int32, (count, groups * high), 0)
        wanted = jnp.where(at - 0 * high < pairs, at + group * pairs, -1)
        for slot, other in enumerate(others):
            inside = at - (slot + 1) * high
            wanted = jnp.where(
                inside >= 0, jnp.where(inside < pairs, inside + other * pairs, -1), wanted)
        gather_pairs = jnp.where(wanted == line, 1.0, 0.0).astype(BF16)
        at = lax.broadcasted_iota(jnp.int32, (2 * high, count), 0)
        line = lax.broadcasted_iota(jnp.int32, (2 * high, count), 1)
        for which, matrix in enumerate((metric, active)):
            spaced = jnp.dot(matrix[...], gather_pairs, preferred_element_type=F32).astype(BF16)
            for kind in range(2):
                other = (left, right)[kind]
                wanted = jnp.where(at < high, at + group * pairs, at - high + other * pairs)
                kept = jnp.where(at < high, at, at - high) < pairs
                choose = jnp.where((wanted == line) & kept, 1.0, 0.0).astype(BF16)
                mats[kind, pl.ds(2 * high * which, 2 * high)] = jnp.dot(
                    choose, spaced, preferred_element_type=F32).astype(BF16)
        at = lax.broadcasted_iota(jnp.int32, fock.shape, 0)
        line = lax.broadcasted_iota(jnp.int32, fock.shape, 1)
        diagonal = jnp.where(at == line, fock[...].astype(F32), 0.0)
        trace = jnp.sum(jnp.sum(diagonal, axis=0, keepdims=True), axis=1, keepdims=True)
        row_sums[0] = jnp.broadcast_to((2.0 / width) * trace, (8, LANES))

    def prepare_spread():
        at = lax.broadcasted_iota(jnp.int32, (width, peers * tall), 0)
        line = lax.broadcasted_iota(jnp.int32, (width, peers * tall), 1)
        across = jnp.where(at + (tall - rows) * (at // rows) == line, 1.0, 0.0).astype(BF16)
        at = lax.broadcasted_iota(jnp.int32, (peers * tall, width), 1)
        line = lax.broadcasted_iota(jnp.int32, (peers * tall, width), 0)
        down = jnp.where(at + (tall - rows) * (at // rows) == line, 1.0, 0.0).astype(BF16)
        half = jnp.dot(fock[...], across, preferred_element_type=F32).astype(BF16)
        spread[...] = jnp.dot(down, half, preferred_element_type=F32).astype(BF16)

    def pass_rows(c):
        settle_rows(c, 0)
        for copy in row_forwards(c):
            copy.start()

    def mix(c):
        shift = row_sums[0, 0:1, 0:1]
        settle_rows(c, 1)
        settle_rows(c, 2)
        for kind in range(2):
            place = 3 * kind
            block = jnp.concatenate([
                jnp.concatenate(
                    [own[c, place, j]] + [gathered[c, kind, slot, j] for slot in range(groups - 1)], axis=0)
                for j in range(part)], axis=1)
            both = jnp.dot(mats[kind], block, preferred_element_type=F32)
            weighted = both[:2 * high]
            half = weighted.astype(BF16)
            rest = (both[2 * high:] - shift * (weighted - half.astype(F32))).astype(BF16)
            for field, value in enumerate((half, rest)):
                for j in range(part):
                    some = slice(LANES * j, LANES * (j + 1))
                    fields[c, place, field, j] = value[:high, some]
                    leaving[c, kind, field, j] = value[high:, some]
            field_copy(c, 0, kind).start()

    def send_active(c, carry):
        for kind in range(2):
            field_copy(c, 1, kind).start()
        return carry

    def turn(c, p):
        first = quarter(p) * part
        for j in range(part):
            wide[pl.ds(first + j, high, stride=tall)] = fields[c, p, 0, j].astype(F32)

    def send_image(c):
        turn(c, 0)
        turn(c, 3)
        field_copy(c, 0, 0).wait_recv()
        turn(c, 1)
        field_copy(c, 0, 1).wait_recv()
        turn(c, 2)

        def narrow(b, carry):
            image[c, pl.ds(b * depth, depth)] = wide[
                pl.ds(pl.multiple_of(b * depth * tall, 8), depth * tall)].astype(BF16).reshape(depth, tall, LANES)
            return carry

        lax.fori_loop(0, pairs // depth, narrow, 0)

        def send(step, carry):
            forward(c, peer_at(step)).start()
            return carry

        lax.fori_loop(1, peers, send, 0)
        for j in range(spares):
            owner = stride * j + spare_place(c)

            @pl.when(owner != me)
            def _(j=j, owner=owner):
                spare_forward(c, j, owner).start()

            @pl.when(owner == me)
            def _(j=j):
                held[c, share, me] = image[c, share * peers + j]

        held[c, pl.ds(0, share), me] = image[c, pl.ds(me * share, share)]

    def apply_fock(c):
        settle(held.at[c, pl.ds(0, share), pl.ds(0, peers - 1), real], landed.at[c])
        block = jnp.concatenate([held[c, i].reshape(peers * tall, LANES) for i in range(share)], axis=1)
        product = jnp.dot(spread[...], block, preferred_element_type=F32).astype(BF16)
        for i in range(share):
            made[c, i] = product[:, LANES * i:LANES * (i + 1)].reshape(peers, tall, LANES)

        def send(step, carry):
            backward(c, peer_at(step)).start()
            return carry

        lax.fori_loop(1, peers, send, 0)
        back[c, pl.ds(me * share, share)] = made[c, pl.ds(0, share), me]

        @pl.when(owns_spare(c))
        def _():
            settle(held.at[c, share, pl.ds(0, peers - 1), real], spare_landed.at[c])
            one = jnp.dot(spread[...], held[c, share].reshape(peers * tall, LANES), preferred_element_type=F32)
            made[c, share] = one.astype(BF16).reshape(peers, tall, LANES)

            def send_spare(step, carry):
                spare_backward(c, peer_at(step)).start()
                return carry

            lax.fori_loop(1, peers, send_spare, 0)
            back[c, share * peers + me // stride] = made[c, share, me]

    def apply_right():
        def block(p, carry):
            shift = row_sums[0, 0:1, 0:1]
            image_rows = jnp.concatenate(
                [fields[c, p, 0].reshape(part * high, LANES) for c in range(chunks)], axis=1)
            product = jnp.dot(image_rows, fock[...], preferred_element_type=F32)
            for c in range(chunks):
                sigma[c, p] = product[:, LANES * c:LANES * (c + 1)] - shift * fields[c, p, 0].reshape(
                    part * high, LANES).astype(F32)
            return carry

        lax.fori_loop(0, groups, block, 0)

    send_early_rows(0)
    send_late_rows(0)
    prepare_mix()
    pass_rows(0)
    send_early_rows(1)

    def tick(n, carry):
        def stage(c, run):
            @pl.when((c >= 0) & (c < chunks))
            def _():
                run(c)

        mix(n)
        stage(n + 1, send_late_rows)
        stage(n + 1, pass_rows)
        stage(n + 2, send_early_rows)

        @pl.when(n == 0)
        def _():
            prepare_spread()

        @pl.when(n == chunks - 2)
        def _():
            lax.fori_loop(0, 2, send_active, 0)

        @pl.when(n == chunks - 1)
        def _():
            lax.fori_loop(2, chunks, send_active, 0)

        stage(jnp.where(n < chunks - 2, n - 1, -1), apply_fock)

        send_image(n)

        @pl.when(n == chunks - 1)
        def _():
            apply_right()

        stage(jnp.where(n < chunks - 2, -1, n - 1), apply_fock)
        return carry

    lax.fori_loop(0, chunks, tick, 0)
    apply_fock(chunks - 1)

    zero = jnp.zeros((8, LANES), F32)

    def combine(c, sums):
        settle(gathered.at[c, :, :, :, real_pairs], row_sent.at[c])
        settle(own.at[c, pl.ds(0, 2), :, real_pairs], active_landed.at[c])
        settle(back.at[c, pl.ds(0, share * (peers - 1)), real], back_landed.at[c])
        settle_spares(c, back, back_spare_landed)

        def widen(b, carry):
            wide[pl.ds(pl.multiple_of(b * depth * tall, 8), depth * tall)] = back[
                c, pl.ds(b * depth, depth)].astype(F32).reshape(depth * tall, LANES)
            return carry

        lax.fori_loop(0, pairs // depth, widen, 0)

        def block(p, sums):
            first = quarter(p) * part
            for j in range(part):
                at = pl.ds(high * j, high)
                x = own[c, p, j].astype(F32)
                w = fields[c, p, 0, j].astype(F32)
                s = sigma[c, p, at] + fields[c, p, 1, j].astype(F32) + wide[pl.ds(first + j, high, stride=tall)]
                sigma[c, p, at] = s
                products = (x * s, x * w, s * s, s * w, w * w)
                sums = tuple(
                    total + jnp.sum(term.reshape(high // 8, 8, LANES), axis=0)
                    for total, term in zip(sums, products))
            return sums

        return lax.fori_loop(0, groups, block, sums)

    sums = lax.fori_loop(0, chunks, combine, (zero,) * 5)
    lane = lax.broadcasted_iota(jnp.int32, (8, LANES), 1)
    packed = zero
    for q, total in enumerate(sums):
        one = jnp.sum(jnp.sum(total, axis=0, keepdims=True), axis=1, keepdims=True)
        packed = jnp.where(lane == q, one, packed)

    def sum_all(phase, value, count, place):
        row_sums[1 + phase] = value
        mine = me if phase == 0 else group

        def copy(other, slot):
            return pltpu.make_async_remote_copy(
                src_ref=row_sums.at[1 + phase], dst_ref=sum_slots.at[phase, slot],
                send_sem=sum_sent.at[phase], recv_sem=sum_landed.at[phase],
                device_id=place(other), device_id_type=MESH)

        def send(step, carry):
            copy(lax.rem(mine + step, count), mine).start()
            return carry

        lax.fori_loop(1, count, send, 0)
        sum_slots[phase, mine] = value

        settle(sum_slots.at[phase, pl.ds(0, count - 1)], sum_landed.at[phase])
        return jnp.sum(sum_slots[phase, pl.ds(0, count)], axis=0)

    packed = sum_all(0, packed, peers, lambda other: (group, other))
    packed = sum_all(1, packed, groups, lambda other: (other, me))
    numer, denom, ss, sw, ww = (packed[0:1, q:q + 1] for q in range(5))
    ratio = numer / denom
    norm = (ss - 2.0 * ratio * sw + ratio * ratio * ww) / denom
    stats_ref[...] = jnp.where(lane == 0, ratio + row_sums[0], norm)

    def store(c, p):
        return pltpu.make_async_copy(
            own.at[c, p, :, real_pairs], out_ref.at[pl.ds(quarter(p) * part, part), :, columns(c)], stored.at[c])

    def finish(c, carry):
        def block(p, carry):
            w = fields[c, p, 0].reshape(part * high, LANES).astype(F32)
            own[c, p] = (sigma[c, p] - ratio * w).astype(BF16).reshape(part, high, LANES)
            store(c, p).start()
            return carry

        lax.fori_loop(0, groups, block, 0)
        return carry

    lax.fori_loop(0, chunks, finish, 0)

    def drain(c, carry):
        settle(leaving.at[c, :, :, :, real_pairs], field_sent.at[c])
        settle(image.at[c, pl.ds(0, share * (peers - 1)), real], sent.at[c])
        settle(made.at[c, pl.ds(0, share), pl.ds(0, peers - 1), real], back_sent.at[c])
        settle_spares(c, image, spare_sent)

        @pl.when(owns_spare(c))
        def _():
            settle(made.at[c, share, pl.ds(0, peers - 1), real], back_spare_sent.at[c])

        settle(own.at[c, :, :, real_pairs], stored.at[c])
        return carry

    lax.fori_loop(0, chunks, drain, 0)
    for phase, count in enumerate((peers, groups)):
        settle(sum_slots.at[phase, pl.ds(0, count - 1)], sum_sent.at[phase])


def local(amplitudes, virtual_fock_block, metric, active_block):
    pairs, rows, width = amplitudes.shape
    peers, groups = lax.axis_size("virt"), lax.axis_size("act")
    chunks = width // LANES
    tall, high = round_up(rows, 8), round_up(pairs, 8)
    part = rows // groups
    items = pairs // peers + 1
    anywhere = pl.BlockSpec(memory_space=pl.ANY)
    dma = pltpu.SemaphoreType.DMA

    def half(*shape):
        return pltpu.VMEM(shape, BF16)

    def full(*shape):
        return pltpu.VMEM(shape, F32)

    resid, stats = pl.pallas_call(
        functools.partial(sigma_kernel, groups, peers),
        out_shape=[
            jax.ShapeDtypeStruct((rows, pairs, width), BF16),
            jax.ShapeDtypeStruct((8, LANES), F32),
        ],
        in_specs=[anywhere] * 4,
        out_specs=[anywhere, pl.BlockSpec(memory_space=pltpu.VMEM)],
        scratch_shapes=[
            half(chunks, groups, part, high, LANES),
            half(*virtual_fock_block.shape), half(*metric.shape), half(*active_block.shape),
            half(peers * tall, peers * tall),
            half(2, groups * high, groups * high),
            half(chunks, 2, groups - 1, part, high, LANES),
            half(chunks, groups, 2, part, high, LANES),
            half(chunks, 2, 2, part, high, LANES),
            full(high * tall, LANES),
            half(chunks, pairs, tall, LANES),
            half(chunks, items, peers, tall, LANES),
            half(chunks, items, peers, tall, LANES),
            half(chunks, pairs, tall, LANES),
            full(chunks, groups, part * high, LANES),
            full(3, 8, LANES),
            full(2, peers, 8, LANES),
            dma((chunks,)), dma((3,)), dma((chunks,)), dma((chunks, 3)), dma((chunks,)), dma((chunks, 2)), dma((chunks,)),
        ] + [dma((chunks,))] * 9 + [dma((2,))] * 2,
        compiler_params=pltpu.CompilerParams(
            collective_id=1, has_side_effects=True, vmem_limit_bytes=62 * 2**20),
    )(jnp.transpose(amplitudes, (1, 0, 2)), virtual_fock_block, metric, active_block)
    return jnp.transpose(resid, (1, 0, 2)), stats[0, 0], stats[0, 1]


def solution(mesh):
    return jax.shard_map(
        local,
        mesh=mesh,
        in_specs=(P("act", "virt", None), P(), P(), P()),
        out_specs=(P("act", "virt", None), P(), P()),
        check_vma=False,
    )
```

time: 158 us -> 115 us (0.73)
  Pallas kernels: 148 us -> 110 us
  local copies, waits for them, and re-layouts: 8.89 us -> 4.83 us
    pallas_call x1, Pallas kernels: 148 us -> 110 us  [local(): pl.pallas_call(functools.partial(sigma_kernel, groups, peers), out_shape=...]
    unnamed x2 -> x1, local copies, waits for them, and re-layouts: 7.55 us -> 3.48 us
where the time goes in v2:
time: 115 us
  Pallas kernels  110 us (96%)
  local copies, waits for them, and re-layouts  4.83 us (4%)
    pallas_call x1, Pallas kernels, local(): pl.pallas_call(functools.partial(sigma_kernel, groups, peers), out_shape=...  110 us
    unnamed x1, local copies, waits for them, and re-layouts  3.48 us

profile of v2, /device:TPU:1, one launch (start us, length us, event | category | flops | bytes accessed | tf_op | source)
XLA Modules:
  0.0 115.2 jit_solution(15492547579557611465)
XLA Ops:
  0.6 109.8 %shard_map.67 = (bf16[20,100,640]{2,1,0:T(8,128)(2,1)}, f32[8,128]{1,0:T(8,128)}) custom-call(bf16[20,100,640]{2,1,0:T(8,128)(2,1)} %bitcast.4, bf16[640,640]{1,0:T(8,128)(2,1)} %fock_ref.1, bf16[400,400]{1,0:T(8,128)(2,1)} %metric_ref.1, bf16[400,400]{1,0:T(8,128)(2,1)} %active_ref.1), custom_call_target="tpu_custom_call" | custom-call | tf_op jit(solution)/shard_map/pallas_call | solution.py:477
  110.4 1.3 %fusion = (f32[1,1]{1,0:T(1,128)}, f32[1,1]{1,0:T(1,128)}) fusion(f32[8,128]{1,0:T(8,128)} %get-tuple-element.6), kind=kLoop, calls=%fused_computation | loop fusion | bytes 16 | tf_op jit(solution)/shard_map/slice | solution.py:506
  111.7 3.5 %copy.8 = bf16[100,20,640]{2,0,1:T(8,128)(2,1)} copy(bf16[100,20,640]{2,0,1:T(8,128)(2,1)} %bitcast.5) | data formatting | bytes 5120000

commit v3 on v2

--- a/solution.py
+++ b/solution.py
@@ -22,7 +22,7 @@
                  loaded, small_loaded, row_sent, row_landed, field_sent, field_landed, active_landed,
                  sent, landed, spare_sent, spare_landed,
                  back_sent, back_landed, back_spare_sent, back_spare_landed,
-                 stored, sum_sent, sum_landed):
+                 sum_sent, sum_landed):
     group, me = lax.axis_index("act"), lax.axis_index("virt")
     chunks, pairs, tall = image.shape[0], image.shape[1], image.shape[2]
     rows, width = x_ref.shape[0], x_ref.shape[2]
@@ -328,35 +328,26 @@
             def _():
                 run(c)
 
+        def only(k, run):
+            @pl.when(n == k)
+            def _():
+                run()
+
         mix(n)
         stage(n + 1, send_late_rows)
         stage(n + 1, pass_rows)
         stage(n + 2, send_early_rows)
-
-        @pl.when(n == 0)
-        def _():
-            prepare_spread()
-
-        @pl.when(n == chunks - 2)
-        def _():
-            lax.fori_loop(0, 2, send_active, 0)
-
-        @pl.when(n == chunks - 1)
-        def _():
-            lax.fori_loop(2, chunks, send_active, 0)
-
-        stage(jnp.where(n < chunks - 2, n - 1, -1), apply_fock)
-
+        only(0, prepare_spread)
+        stage(jnp.where(n < chunks - 3, n - 1, -1), apply_fock)
         send_image(n)
 
-        @pl.when(n == chunks - 1)
-        def _():
-            apply_right()
-
-        stage(jnp.where(n < chunks - 2, -1, n - 1), apply_fock)
+        only(chunks - 2, lambda: lax.fori_loop(0, 2, send_active, 0))
+        only(chunks - 1, lambda: lax.fori_loop(2, chunks, send_active, 0))
+        stage(jnp.where(n < chunks - 3, -1, n - 1), apply_fock)
         return carry
 
     lax.fori_loop(0, chunks, tick, 0)
+    apply_right()
     apply_fock(chunks - 1)
 
     zero = jnp.zeros((8, LANES), F32)
@@ -424,15 +415,11 @@
     norm = (ss - 2.0 * ratio * sw + ratio * ratio * ww) / denom
     stats_ref[...] = jnp.where(lane == 0, ratio + row_sums[0], norm)
 
-    def store(c, p):
-        return pltpu.make_async_copy(
-            own.at[c, p, :, real_pairs], out_ref.at[pl.ds(quarter(p) * part, part), :, columns(c)], stored.at[c])
-
     def finish(c, carry):
         def block(p, carry):
             w = fields[c, p, 0].reshape(part * high, LANES).astype(F32)
-            own[c, p] = (sigma[c, p] - ratio * w).astype(BF16).reshape(part, high, LANES)
-            store(c, p).start()
+            resid = (sigma[c, p] - ratio * w).astype(BF16).reshape(part, high, LANES)
+            out_ref[pl.ds(quarter(p) * part, part), :, columns(c)] = resid[:, :pairs]
             return carry
 
         lax.fori_loop(0, groups, block, 0)
@@ -450,7 +437,6 @@
         def _():
             settle(made.at[c, share, pl.ds(0, peers - 1), real], back_spare_sent.at[c])
 
-        settle(own.at[c, :, :, real_pairs], stored.at[c])
         return carry
 
     lax.fori_loop(0, chunks, drain, 0)
@@ -480,8 +466,8 @@
             jax.ShapeDtypeStruct((rows, pairs, width), BF16),
             jax.ShapeDtypeStruct((8, LANES), F32),
         ],
-        in_specs=[anywhere] * 4,
-        out_specs=[anywhere, pl.BlockSpec(memory_space=pltpu.VMEM)],
+        in_specs=[pl.BlockSpec(memory_space=pltpu.HBM)] * 4,
+        out_specs=[pl.BlockSpec(memory_space=pltpu.VMEM)] * 2,
         scratch_shapes=[
             half(chunks, groups, part, high, LANES),
             half(*virtual_fock_block.shape), half(*metric.shape), half(*active_block.shape),
@@ -499,10 +485,11 @@
             full(3, 8, LANES),
             full(2, peers, 8, LANES),
             dma((chunks,)), dma((3,)), dma((chunks,)), dma((chunks, 3)), dma((chunks,)), dma((chunks, 2)), dma((chunks,)),
-        ] + [dma((chunks,))] * 9 + [dma((2,))] * 2,
+        ] + [dma((chunks,))] * 8 + [dma((2,))] * 2,
         compiler_params=pltpu.CompilerParams(
-            collective_id=1, has_side_effects=True, vmem_limit_bytes=62 * 2**20),
-    )(jnp.transpose(amplitudes, (1, 0, 2)), virtual_fock_block, metric, active_block)
+            collective_id=1, has_side_effects=True, vmem_limit_bytes=48 * 2**20),
+    )(*(pltpu.with_memory_space_constraint(array, pltpu.HBM) for array in (
+        jnp.transpose(amplitudes, (1, 0, 2)), virtual_fock_block, metric, active_block)))
     return jnp.transpose(resid, (1, 0, 2)), stats[0, 0], stats[0, 1]
 
 

time: 115 us -> 109 us (0.948)
  Pallas kernels: 110 us -> 106 us
  local copies, waits for them, and re-layouts: 4.83 us -> 2.09 us
    pallas_call x1, Pallas kernels: 110 us -> 106 us  [local(): pl.pallas_call(functools.partial(sigma_kernel, groups, peers), out_shape=...]
    unnamed x1, local copies, waits for them, and re-layouts: 3.48 us -> 1.51 us
where the time goes in v3:
time: 109 us
  Pallas kernels  106 us (97%)
  local copies, waits for them, and re-layouts  2.09 us (2%)
    pallas_call x1, Pallas kernels, local(): pl.pallas_call(functools.partial(sigma_kernel, groups, peers), out_shape=...  106 us

profile of v3, /device:TPU:1, one launch (start us, length us, event | category | flops | bytes accessed | tf_op | source)
XLA Modules:
  0.0 108.6 jit_solution(13227359082054649919)
XLA Ops:
  0.6 105.9 %shard_map.67 = (bf16[20,100,640]{2,1,0:T(8,128)(2,1)S(1)}, f32[8,128]{1,0:T(8,128)S(1)}) custom-call(bf16[20,100,640]{2,1,0:T(8,128)(2,1)} %bitcast.5, bf16[640,640]{1,0:T(8,128)(2,1)} %fock_ref.1, bf16[400,400]{1,0:T(8,128)(2,1)} %metric_ref.1, bf16[400,400]{1,0:T(8,128)(2,1)} %active_ref.1), custom_call_target="tpu_custom_call" | custom-call | tf_op jit(solution)/shard_map/pallas_call | solution.py:463
  106.5 0.6 fusion
  107.1 1.5 %copy.8 = bf16[100,20,640]{2,0,1:T(8,128)(2,1)} copy(bf16[100,20,640]{2,0,1:T(8,128)(2,1)S(1)} %bitcast.4) | data formatting | bytes 5120000

commit v4 on v3

--- a/solution.py
+++ b/solution.py
@@ -36,6 +36,7 @@
     real = pl.ds(0, rows)
     real_pairs = pl.ds(0, pairs)
     depth = 10
+    last = chunks - 1
 
     def quarter(p):
         return lax.rem(group + p, groups)
@@ -65,12 +66,17 @@
 
     def clear(c, carry):
         held[c, :, :, extra] = jnp.zeros(held.shape[1:3] + (tall - rows, LANES), BF16)
+        fields[c, :, :, :, beyond] = jnp.zeros(fields.shape[1:4] + (high - pairs, LANES), BF16)
+        return carry
+
+    def clear_rows(c, carry):
         gathered[c, :, :, :, beyond] = jnp.zeros(gathered.shape[1:4] + (high - pairs, LANES), BF16)
         own[c, :, :, beyond] = jnp.zeros(own.shape[1:3] + (high - pairs, LANES), BF16)
-        fields[c, :, :, :, beyond] = jnp.zeros(fields.shape[1:4] + (high - pairs, LANES), BF16)
         return carry
 
     lax.fori_loop(0, chunks, clear, 0)
+    lax.fori_loop(0, chunks + 1, clear_rows, 0)
+    back[last, :, extra] = jnp.zeros((pairs, tall - rows, LANES), BF16)
 
     def greet(step, carry):
         pl.semaphore_signal(barrier, inc=1, device_id=(group, lax.rem(me + step, peers)), device_id_type=MESH)
@@ -160,7 +166,10 @@
         return lax.rem(me, stride) == spare_place(c)
 
     def send_early_rows(c):
-        settle(own.at[c, :, :, real_pairs], loaded.at[c])
+        @pl.when(c < last)
+        def _():
+            settle(own.at[c, :, :, real_pairs], loaded.at[c])
+
         for copy in early_rows(c):
             copy.start()
 
@@ -212,20 +221,28 @@
         for copy in row_forwards(c):
             copy.start()
 
-    def mix(c):
+    def block_of(c, kind):
+        return jnp.concatenate([
+            jnp.concatenate(
+                [own[c, 3 * kind, j]] + [gathered[c, kind, slot, j] for slot in range(groups - 1)], axis=0)
+            for j in range(part)], axis=1)
+
+    def mix(c, applied=None):
         shift = row_sums[0, 0:1, 0:1]
         settle_rows(c, 1)
         settle_rows(c, 2)
+        if applied is not None:
+            settle_rows(applied, 1)
+            settle_rows(applied, 2)
         for kind in range(2):
             place = 3 * kind
-            block = jnp.concatenate([
-                jnp.concatenate(
-                    [own[c, place, j]] + [gathered[c, kind, slot, j] for slot in range(groups - 1)], axis=0)
-                for j in range(part)], axis=1)
-            both = jnp.dot(mats[kind], block, preferred_element_type=F32)
+            both = jnp.dot(mats[kind], block_of(c, kind), preferred_element_type=F32)
             weighted = both[:2 * high]
             half = weighted.astype(BF16)
-            rest = (both[2 * high:] - shift * (weighted - half.astype(F32))).astype(BF16)
+            rest = both[2 * high:] - shift * (weighted - half.astype(F32))
+            if applied is not None:
+                rest += jnp.dot(mats[kind, :2 * high], block_of(applied, kind), preferred_element_type=F32)
+            rest = rest.astype(BF16)
             for field, value in enumerate((half, rest)):
                 for j in range(part):
                     some = slice(LANES * j, LANES * (j + 1))
@@ -238,19 +255,27 @@
             field_copy(c, 1, kind).start()
         return carry
 
-    def turn(c, p):
+    def turn(source, p):
         first = quarter(p) * part
         for j in range(part):
-            wide[pl.ds(first + j, high, stride=tall)] = fields[c, p, 0, j].astype(F32)
+            wide[pl.ds(first + j, high, stride=tall)] = source[j].astype(F32)
 
     def send_image(c):
-        turn(c, 0)
-        turn(c, 3)
+        turn(fields.at[c, 0, 0], 0)
+        turn(fields.at[c, 3, 0], 3)
         field_copy(c, 0, 0).wait_recv()
-        turn(c, 1)
+        turn(fields.at[c, 1, 0], 1)
         field_copy(c, 0, 1).wait_recv()
-        turn(c, 2)
-
+        turn(fields.at[c, 2, 0], 2)
+        send_slabs(c)
+
+    def send_trial(c):
+        settle(own.at[c, :, :, real_pairs], loaded.at[c])
+        for p in range(groups):
+            turn(own.at[c, p], p)
+        send_slabs(c)
+
+    def send_slabs(c):
         def narrow(b, carry):
             image[c, pl.ds(b * depth, depth)] = wide[
                 pl.ds(pl.multiple_of(b * depth * tall, 8), depth * tall)].astype(BF16).reshape(depth, tall, LANES)
@@ -302,6 +327,24 @@
 
             lax.fori_loop(1, peers, send_spare, 0)
             back[c, share * peers + me // stride] = made[c, share, me]
+
+    def widen_back(c):
+        settle(back.at[c, pl.ds(0, share * (peers - 1)), real], back_landed.at[c])
+        settle_spares(c, back, back_spare_landed)
+
+        def widen(b, carry):
+            wide[pl.ds(pl.multiple_of(b * depth * tall, 8), depth * tall)] = back[
+                c, pl.ds(b * depth, depth)].astype(F32).reshape(depth * tall, LANES)
+            return carry
+
+        lax.fori_loop(0, pairs // depth, widen, 0)
+
+    def turn_applied():
+        widen_back(last)
+        for p in range(groups):
+            first = quarter(p) * part
+            for j in range(part):
+                own[chunks, p, j] = wide[pl.ds(first + j, high, stride=tall)].astype(BF16)
 
     def apply_right():
         def block(p, carry):
@@ -318,52 +361,58 @@
 
     send_early_rows(0)
     send_late_rows(0)
+    send_trial(last)
     prepare_mix()
     pass_rows(0)
     send_early_rows(1)
+    prepare_spread()
+    apply_fock(last)
 
     def tick(n, carry):
-        def stage(c, run):
-            @pl.when((c >= 0) & (c < chunks))
-            def _():
-                run(c)
-
-        def only(k, run):
-            @pl.when(n == k)
-            def _():
-                run()
-
         mix(n)
-        stage(n + 1, send_late_rows)
-        stage(n + 1, pass_rows)
-        stage(n + 2, send_early_rows)
-        only(0, prepare_spread)
-        stage(jnp.where(n < chunks - 3, n - 1, -1), apply_fock)
+        send_late_rows(n + 1)
+        pass_rows(n + 1)
+        send_early_rows(n + 2)
+
+        @pl.when(n == 1)
+        def _():
+            apply_fock(0)
+
         send_image(n)
 
-        only(chunks - 2, lambda: lax.fori_loop(0, 2, send_active, 0))
-        only(chunks - 1, lambda: lax.fori_loop(2, chunks, send_active, 0))
-        stage(jnp.where(n < chunks - 3, -1, n - 1), apply_fock)
-        return carry
-
-    lax.fori_loop(0, chunks, tick, 0)
+        @pl.when(n == 1)
+        def _():
+            turn_applied()
+
+        @pl.when(n > 1)
+        def _():
+            apply_fock(n - 1)
+
+        return carry
+
+    lax.fori_loop(0, last, tick, 0)
+    send_late_rows(chunks)
+    pass_rows(chunks)
+    lax.fori_loop(0, 2, send_active, 0)
+    apply_fock(last - 1)
+    mix(last, chunks)
+    lax.fori_loop(2, chunks, send_active, 0)
+    for kind in range(2):
+        field_copy(last, 0, kind).wait_recv()
     apply_right()
-    apply_fock(chunks - 1)
 
     zero = jnp.zeros((8, LANES), F32)
 
     def combine(c, sums):
-        settle(gathered.at[c, :, :, :, real_pairs], row_sent.at[c])
         settle(own.at[c, pl.ds(0, 2), :, real_pairs], active_landed.at[c])
-        settle(back.at[c, pl.ds(0, share * (peers - 1)), real], back_landed.at[c])
-        settle_spares(c, back, back_spare_landed)
-
-        def widen(b, carry):
-            wide[pl.ds(pl.multiple_of(b * depth * tall, 8), depth * tall)] = back[
-                c, pl.ds(b * depth, depth)].astype(F32).reshape(depth * tall, LANES)
-            return carry
-
-        lax.fori_loop(0, pairs // depth, widen, 0)
+
+        @pl.when(c < last)
+        def _():
+            widen_back(c)
+
+        @pl.when(c == last)
+        def _():
+            wide[...] = jnp.zeros(wide.shape, F32)
 
         def block(p, sums):
             first = quarter(p) * part
@@ -428,6 +477,7 @@
     lax.fori_loop(0, chunks, finish, 0)
 
     def drain(c, carry):
+        settle(gathered.at[c, :, :, :, real_pairs], row_sent.at[c])
         settle(leaving.at[c, :, :, :, real_pairs], field_sent.at[c])
         settle(image.at[c, pl.ds(0, share * (peers - 1)), real], sent.at[c])
         settle(made.at[c, pl.ds(0, share), pl.ds(0, peers - 1), real], back_sent.at[c])
@@ -440,6 +490,7 @@
         return carry
 
     lax.fori_loop(0, chunks, drain, 0)
+    settle(gathered.at[chunks, :, :, :, real_pairs], row_sent.at[chunks])
     for phase, count in enumerate((peers, groups)):
         settle(sum_slots.at[phase, pl.ds(0, count - 1)], sum_sent.at[phase])
 
@@ -469,11 +520,11 @@
         in_specs=[pl.BlockSpec(memory_space=pltpu.HBM)] * 4,
         out_specs=[pl.BlockSpec(memory_space=pltpu.VMEM)] * 2,
         scratch_shapes=[
-            half(chunks, groups, part, high, LANES),
+            half(chunks + 1, groups, part, high, LANES),
             half(*virtual_fock_block.shape), half(*metric.shape), half(*active_block.shape),
             half(peers * tall, peers * tall),
             half(2, groups * high, groups * high),
-            half(chunks, 2, groups - 1, part, high, LANES),
+            half(chunks + 1, 2, groups - 1, part, high, LANES),
             half(chunks, groups, 2, part, high, LANES),
             half(chunks, 2, 2, part, high, LANES),
             full(high * tall, LANES),
@@ -484,7 +535,7 @@
             full(chunks, groups, part * high, LANES),
             full(3, 8, LANES),
             full(2, peers, 8, LANES),
-            dma((chunks,)), dma((3,)), dma((chunks,)), dma((chunks, 3)), dma((chunks,)), dma((chunks, 2)), dma((chunks,)),
+            dma((chunks,)), dma((3,)), dma((chunks + 1,)), dma((chunks + 1, 3)), dma((chunks,)), dma((chunks, 2)), dma((chunks,)),
         ] + [dma((chunks,))] * 8 + [dma((2,))] * 2,
         compiler_params=pltpu.CompilerParams(
             collective_id=1, has_side_effects=True, vmem_limit_bytes=48 * 2**20),

time: 109 us -> 103 us (0.945)
  Pallas kernels: 106 us -> 101 us
    pallas_call x1, Pallas kernels: 106 us -> 101 us  [local(): pl.pallas_call(functools.partial(sigma_kernel, groups, peers), out_shape=...]
where the time goes in v4:
time: 103 us
  Pallas kernels  101 us (98%)
  local copies, waits for them, and re-layouts  2.09 us (2%)
    pallas_call x1, Pallas kernels, local(): pl.pallas_call(functools.partial(sigma_kernel, groups, peers), out_shape=...  101 us

profile of v4, /device:TPU:1, one launch (start us, length us, event | category | flops | bytes accessed | tf_op | source)
XLA Modules:
  0.0 103.3 jit_solution(1802836939864804451)
XLA Ops:
  0.6 100.6 %shard_map.67 = (bf16[20,100,640]{2,1,0:T(8,128)(2,1)S(1)}, f32[8,128]{1,0:T(8,128)S(1)}) custom-call(bf16[20,100,640]{2,1,0:T(8,128)(2,1)} %bitcast.5, bf16[640,640]{1,0:T(8,128)(2,1)} %fock_ref.1, bf16[400,400]{1,0:T(8,128)(2,1)} %metric_ref.1, bf16[400,400]{1,0:T(8,128)(2,1)} %active_ref.1), custom_call_target="tpu_custom_call" | custom-call | tf_op jit(solution)/shard_map/pallas_call | solution.py:514
  101.2 0.6 fusion
  101.8 1.5 %copy.8 = bf16[100,20,640]{2,0,1:T(8,128)(2,1)} copy(bf16[100,20,640]{2,0,1:T(8,128)(2,1)S(1)} %bitcast.4) | data formatting | bytes 5120000

commit v5 on v4

--- a/solution.py
+++ b/solution.py
@@ -56,11 +56,19 @@
             load(c, p).start()
         return carry
 
+    barrier = pltpu.get_barrier_semaphore()
+
+    def greet(step, carry):
+        pl.semaphore_signal(barrier, inc=1, device_id=(group, lax.rem(me + step, peers)), device_id_type=MESH)
+        return carry
+
+    lax.fori_loop(1, peers, greet, 0)
+    for step in range(1, groups):
+        pl.semaphore_signal(barrier, inc=1, device_id=(lax.rem(group + step, groups), me), device_id_type=MESH)
     lax.fori_loop(0, chunks, start_loads, 0)
     for copy in smalls:
         copy.start()
 
-    barrier = pltpu.get_barrier_semaphore()
     extra = pl.ds(rows, tall - rows)
     beyond = pl.ds(pairs, high - pairs)
 
@@ -78,13 +86,6 @@
     lax.fori_loop(0, chunks + 1, clear_rows, 0)
     back[last, :, extra] = jnp.zeros((pairs, tall - rows, LANES), BF16)
 
-    def greet(step, carry):
-        pl.semaphore_signal(barrier, inc=1, device_id=(group, lax.rem(me + step, peers)), device_id_type=MESH)
-        return carry
-
-    lax.fori_loop(1, peers, greet, 0)
-    for step in range(1, groups):
-        pl.semaphore_signal(barrier, inc=1, device_id=(lax.rem(group + step, groups), me), device_id_type=MESH)
     for q in range(tall - rows):
         wide[pl.ds(rows + q, high, stride=tall)] = jnp.zeros((high, LANES), F32)
     pl.semaphore_wait(barrier, peers + groups - 2)
@@ -227,28 +228,38 @@
                 [own[c, 3 * kind, j]] + [gathered[c, kind, slot, j] for slot in range(groups - 1)], axis=0)
             for j in range(part)], axis=1)
 
-    def mix(c, applied=None):
+    def mix(c):
         shift = row_sums[0, 0:1, 0:1]
         settle_rows(c, 1)
         settle_rows(c, 2)
-        if applied is not None:
-            settle_rows(applied, 1)
-            settle_rows(applied, 2)
         for kind in range(2):
             place = 3 * kind
             both = jnp.dot(mats[kind], block_of(c, kind), preferred_element_type=F32)
             weighted = both[:2 * high]
             half = weighted.astype(BF16)
-            rest = both[2 * high:] - shift * (weighted - half.astype(F32))
-            if applied is not None:
-                rest += jnp.dot(mats[kind, :2 * high], block_of(applied, kind), preferred_element_type=F32)
-            rest = rest.astype(BF16)
+            rest = (both[2 * high:] - shift * (weighted - half.astype(F32))).astype(BF16)
             for field, value in enumerate((half, rest)):
                 for j in range(part):
                     some = slice(LANES * j, LANES * (j + 1))
                     fields[c, place, field, j] = value[:high, some]
                     leaving[c, kind, field, j] = value[high:, some]
             field_copy(c, 0, kind).start()
+
+    def mix_applied():
+        shift = row_sums[0, 0:1, 0:1]
+        settle_rows(chunks, 1)
+        settle_rows(chunks, 2)
+        for kind in range(2):
+            both = jnp.dot(mats[kind], block_of(last, kind), preferred_element_type=F32)
+            weighted = both[:2 * high]
+            rest = both[2 * high:] - shift * (weighted - weighted.astype(BF16).astype(F32))
+            rest += jnp.dot(mats[kind, :2 * high], block_of(chunks, kind), preferred_element_type=F32)
+            rest = rest.astype(BF16)
+            for j in range(part):
+                some = slice(LANES * j, LANES * (j + 1))
+                fields[last, 3 * kind, 1, j] = rest[:high, some]
+                leaving[last, kind, 1, j] = rest[high:, some]
+            field_copy(last, 1, kind).start()
 
     def send_active(c, carry):
         for kind in range(2):
@@ -365,38 +376,51 @@
     prepare_mix()
     pass_rows(0)
     send_early_rows(1)
+    send_late_rows(1)
     prepare_spread()
     apply_fock(last)
 
     def tick(n, carry):
         mix(n)
-        send_late_rows(n + 1)
         pass_rows(n + 1)
-        send_early_rows(n + 2)
+
+        @pl.when(n < last)
+        def _():
+            send_early_rows(n + 2)
+            send_late_rows(n + 2)
 
         @pl.when(n == 1)
         def _():
             apply_fock(0)
 
-        send_image(n)
+        @pl.when(n < last)
+        def _():
+            send_image(n)
 
         @pl.when(n == 1)
         def _():
             turn_applied()
 
-        @pl.when(n > 1)
+        @pl.when((n > 1) & (n < last))
         def _():
             apply_fock(n - 1)
 
         return carry
 
-    lax.fori_loop(0, last, tick, 0)
-    send_late_rows(chunks)
-    pass_rows(chunks)
-    lax.fori_loop(0, 2, send_active, 0)
+    lax.fori_loop(0, chunks, tick, 0)
+    hurried = lax.rem(me, 2) == 1
+
+    @pl.when(jnp.logical_not(hurried))
+    def _():
+        lax.fori_loop(0, last, send_active, 0)
+
     apply_fock(last - 1)
-    mix(last, chunks)
-    lax.fori_loop(2, chunks, send_active, 0)
+
+    @pl.when(hurried)
+    def _():
+        lax.fori_loop(0, last, send_active, 0)
+
+    mix_applied()
     for kind in range(2):
         field_copy(last, 0, kind).wait_recv()
     apply_right()

time: 103 us -> 100 us (0.971)
  Pallas kernels: 101 us -> 97.4 us
    pallas_call x1, Pallas kernels: 101 us -> 97.4 us  [local(): pl.pallas_call(functools.partial(sigma_kernel, groups, peers), out_shape=...]
where the time goes in v5:
time: 100 us
  Pallas kernels  97.4 us (97%)
  local copies, waits for them, and re-layouts  2.09 us (2%)
    pallas_call x1, Pallas kernels, local(): pl.pallas_call(functools.partial(sigma_kernel, groups, peers), out_shape=...  97.4 us

profile of v5, /device:TPU:1, one launch (start us, length us, event | category | flops | bytes accessed | tf_op | source)
XLA Modules:
  0.0 100.1 jit_solution(8329988773954151014)
XLA Ops:
  0.6 97.4 %shard_map.67 = (bf16[20,100,640]{2,1,0:T(8,128)(2,1)S(1)}, f32[8,128]{1,0:T(8,128)S(1)}) custom-call(bf16[20,100,640]{2,1,0:T(8,128)(2,1)} %bitcast.5, bf16[640,640]{1,0:T(8,128)(2,1)} %fock_ref.1, bf16[400,400]{1,0:T(8,128)(2,1)} %metric_ref.1, bf16[400,400]{1,0:T(8,128)(2,1)} %active_ref.1), custom_call_target="tpu_custom_call" | custom-call | tf_op jit(solution)/shard_map/pallas_call | solution.py:538
  98.0 0.6 fusion
  98.6 1.5 %copy.8 = bf16[100,20,640]{2,0,1:T(8,128)(2,1)} copy(bf16[100,20,640]{2,0,1:T(8,128)(2,1)S(1)} %bitcast.4) | data formatting | bytes 5120000

commit v6 on v5

--- a/solution.py
+++ b/solution.py
@@ -389,21 +389,17 @@
             send_early_rows(n + 2)
             send_late_rows(n + 2)
 
+        @pl.when((n == 1) | (n > 2))
+        def _():
+            apply_fock(jnp.where(n == 1, 0, n - 2))
+
+        @pl.when(n < last)
+        def _():
+            send_image(n)
+
         @pl.when(n == 1)
         def _():
-            apply_fock(0)
-
-        @pl.when(n < last)
-        def _():
-            send_image(n)
-
-        @pl.when(n == 1)
-        def _():
             turn_applied()
-
-        @pl.when((n > 1) & (n < last))
-        def _():
-            apply_fock(n - 1)
 
         return carry
 

time: 100 us -> 101 us (1.010)
  no operation moved by 1% of the time
where the time goes in v6:
time: 101 us
  Pallas kernels  97.8 us (97%)
  local copies, waits for them, and re-layouts  2.09 us (2%)
    pallas_call x1, Pallas kernels, local(): pl.pallas_call(functools.partial(sigma_kernel, groups, peers), out_shape=...  97.8 us

profile of v6, /device:TPU:1, one launch (start us, length us, event | category | flops | bytes accessed | tf_op | source)
XLA Modules:
  0.0 100.5 jit_solution(11076814280528227163)
XLA Ops:
  0.6 97.8 %shard_map.67 = (bf16[20,100,640]{2,1,0:T(8,128)(2,1)S(1)}, f32[8,128]{1,0:T(8,128)S(1)}) custom-call(bf16[20,100,640]{2,1,0:T(8,128)(2,1)} %bitcast.5, bf16[640,640]{1,0:T(8,128)(2,1)} %fock_ref.1, bf16[400,400]{1,0:T(8,128)(2,1)} %metric_ref.1, bf16[400,400]{1,0:T(8,128)(2,1)} %active_ref.1), custom_call_target="tpu_custom_call" | custom-call | tf_op jit(solution)/shard_map/pallas_call | solution.py:534
  98.4 0.6 fusion
  99.0 1.5 %copy.8 = bf16[100,20,640]{2,0,1:T(8,128)(2,1)} copy(bf16[100,20,640]{2,0,1:T(8,128)(2,1)S(1)} %bitcast.4) | data formatting | bytes 5120000
